TPU v7x, 32 devices: a whole 2x2x4 slice. The times are simulated.
32 devices in a mesh: dp: 8 (over z, y), mp: 4 (over x, core).
Axes of the slice: x: 2, y: 2, z: 4, core: 2. Of those that a mesh axis runs over, the one named last changes fastest.
Arguments:
- queries: bfloat16 [64, 64, 128], P('dp', 'mp'), may hold values from -140 to 140
- resident_cache: bfloat16 [64, 256, 8, 128], P('dp', None, 'mp'), may hold values from -6 to 6
- overflow_cache: bfloat16 [8, 8, 8, 128, 8, 128], P('dp', None, None, None, 'mp'), may hold values from -6 to 6
- key_up_weight: bfloat16 [8, 64, 128], P('mp'), may hold values from -0.75 to 0.75
- value_up_weight: bfloat16 [8, 64, 128], P('mp'), may hold values from -0.75 to 0.75
- lengths: int32 [64], replicated, may hold values from 257 to 1024
- routes: int32 [64, 6, 1], replicated, may hold values from 0 to 7; in each aligned block of 48 rows (0 to 47, 48 to 95, ..., all dimensions but the last counted through in order) at most 8 rows name the same one
- out_weight: bfloat16 [8192, 8192], P('mp', 'dp'), may hold values from -0.0625 to 0.0625
Outputs:
- mixed_out: bfloat16 [64, 8192], P('mp', 'dp')
Inputs may be any that keep to these rules, and one draw needn't show every extreme that they name: Among the 48 entries of one sequence group (sequences s with the same s // 8) no group is named more than 8 times; the page named by routes[s, j, 0] lies in the slots of that holding group kept for the group s // 8, at the slot given by ranking. Slots that no entry names hold data that no output reads.
All inputs are finite; a program needn't handle non-finite values.
Results may differ from a plain program's by a relative error of at most 0.0049.
Values may be sent and summed in bfloat16 or wider, within the bound.
No kernel may reach another device: no remote copies, remote signals or barrier semaphores. Data moves between devices by JAX's collectives and lax.ppermute only.
A program may use at most 64 MiB of HBM per device.

v0:
```python
import math

import jax
import jax.numpy as jnp
from jax import lax
from jax.sharding import PartitionSpec as P

very_low = -1e30


def spill_ranks(targets):
    entry_count = targets.shape[-1]
    position = jnp.arange(entry_count, dtype=jnp.int32)
    same_target = targets[..., :, None] == targets[..., None, :]
    earlier = position[None, :] < position[:, None]
    return jnp.sum((same_target & earlier).astype(jnp.int32), axis=-1)


def slot_entries(targets, ranking, wanted, slot_count):
    choices_row = jnp.arange(slot_count, dtype=jnp.int32)
    matches = (targets[:, None, :] == wanted) & (ranking[:, None, :] == choices_row[None, :, None])
    position = jnp.arange(targets.shape[-1], dtype=jnp.int32)
    entries = jnp.sum(jnp.where(matches, position, 0), axis=-1)
    present = jnp.any(matches, axis=-1)
    return (entries, present)


def page_partials(latent_vector, query_rows, token_valid, key_up_weight, value_up_weight):
    key_width = key_up_weight.shape[1]
    score_scale = 1.0 / math.sqrt(key_up_weight.shape[2])
    highest = lax.Precision.HIGHEST
    rebuilt_keys = jnp.einsum(
        "ptkr,krd->ptkd",
        latent_vector[..., :key_width],
        key_up_weight,
        preferred_element_type=jnp.float32,
    )
    scores = jnp.einsum(
        "pkgd,ptkd->pkgt", query_rows.astype(jnp.float32), rebuilt_keys, precision=highest
    )
    scores = scores * score_scale
    token_mask = token_valid[:, None, None, :]
    scores = jnp.where(token_mask, scores, very_low)
    peak_score = jnp.max(scores, axis=-1)
    weights = jnp.where(token_mask, jnp.exp(scores - peak_score[..., None]), 0.0)
    weight_sum = jnp.sum(weights, axis=-1)
    rebuilt_values = jnp.einsum(
        "ptkr,krd->ptkd",
        latent_vector[..., key_width:],
        value_up_weight,
        preferred_element_type=jnp.float32,
    )
    weighted = jnp.einsum("pkgt,ptkd->pkgd", weights, rebuilt_values, precision=highest)
    return (peak_score, weight_sum, weighted)


def merge_parts(home_parts, far_parts, own_sequence, present):
    highest = lax.Precision.HIGHEST
    home_peak, home_sum, home_weighted = home_parts
    far_peak, far_sum, far_weighted = far_parts
    seq_count = home_peak.shape[0]
    member = (own_sequence[:, None] == jnp.arange(seq_count, dtype=jnp.int32)[None, :]) & present[
        :, None
    ]
    member_weight = member.astype(jnp.float32)
    far_best = jnp.max(jnp.where(member[:, :, None, None], far_peak[:, None], very_low), axis=0)
    highest_peak = jnp.maximum(home_peak, far_best)
    item_peak = jnp.einsum("is,skg->ikg", member_weight, highest_peak, precision=highest)
    far_factor = jnp.where(present[:, None, None], jnp.exp(far_peak - item_peak), 0.0)
    home_factor = jnp.exp(home_peak - highest_peak)
    weight_sum = home_sum * home_factor + jnp.einsum(
        "is,ikg->skg", member_weight, far_sum * far_factor, precision=highest
    )
    weighted = home_weighted * home_factor[..., None] + jnp.einsum(
        "is,ikgd->skgd", member_weight, far_weighted * far_factor[..., None], precision=highest
    )
    return weighted / weight_sum[..., None]


def body(
    queries,
    resident_cache,
    overflow_cache,
    key_up_weight,
    value_up_weight,
    lengths,
    routes,
    out_weight,
):
    seq_dev, head_dev, head_size = queries.shape
    kv_heads = key_up_weight.shape[0]
    head_cluster = head_dev // kv_heads
    group_count = lax.axis_size("dp")
    own_group = lax.axis_index("dp")
    slot_count = overflow_cache.shape[2]
    page_size = overflow_cache.shape[3]
    home_tokens = resident_cache.shape[1]
    tail_pages = routes.shape[1]
    item_count = group_count * slot_count
    targets_all = routes[:, :, 0].reshape(group_count, seq_dev * tail_pages)
    ranking_all = spill_ranks(targets_all)
    own_lengths = lax.dynamic_slice_in_dim(lengths, own_group * seq_dev, seq_dev)
    local_queries = queries.reshape(seq_dev, kv_heads, head_cluster, head_size)
    home_valid = jnp.arange(home_tokens, dtype=jnp.int32)[None, :] < own_lengths[:, None]
    home_parts = page_partials(
        resident_cache, local_queries, home_valid, key_up_weight, value_up_weight
    )
    own_targets = lax.dynamic_slice_in_dim(targets_all, own_group, 1)
    own_ranking = lax.dynamic_slice_in_dim(ranking_all, own_group, 1)
    holders = jnp.arange(group_count, dtype=jnp.int32)[:, None, None]
    own_entries, own_present = slot_entries(own_targets, own_ranking, holders, slot_count)
    own_sequence = (own_entries // tail_pages).reshape(item_count)
    page_offsets = jnp.arange(page_size, dtype=jnp.int32)
    all_queries = lax.all_gather(queries, "dp", axis=0, tiled=True)
    entries, present = slot_entries(targets_all, ranking_all, own_group, slot_count)
    sources = jnp.arange(group_count, dtype=jnp.int32)[:, None]
    sequence = sources * seq_dev + entries // tail_pages
    first_token = home_tokens + entries % tail_pages * page_size
    item_valid = (first_token[..., None] + page_offsets < lengths[sequence][..., None]) & present[
        ..., None
    ]
    item_queries = all_queries[sequence.reshape(item_count)].reshape(
        item_count, kv_heads, head_cluster, head_size
    )
    latent_vector = overflow_cache.reshape(item_count, page_size, kv_heads, -1)
    peak_score, weight_sum, weighted = page_partials(
        latent_vector,
        item_queries,
        item_valid.reshape(item_count, page_size),
        key_up_weight,
        value_up_weight,
    )
    peak_score, weight_sum, weighted = (
        lax.all_to_all(
            peak_score.reshape(group_count, slot_count, kv_heads, head_cluster),
            "dp",
            split_axis=0,
            concat_axis=0,
            tiled=True,
        ),
        lax.all_to_all(
            weight_sum.reshape(group_count, slot_count, kv_heads, head_cluster),
            "dp",
            split_axis=0,
            concat_axis=0,
            tiled=True,
        ),
        lax.all_to_all(
            weighted.reshape(group_count, slot_count, kv_heads, head_cluster, head_size),
            "dp",
            split_axis=0,
            concat_axis=0,
            tiled=True,
        ),
    )
    far_parts = (
        peak_score.reshape(item_count, kv_heads, head_cluster),
        weight_sum.reshape(item_count, kv_heads, head_cluster),
        weighted.reshape(item_count, kv_heads, head_cluster, head_size),
    )
    attended = merge_parts(home_parts, far_parts, own_sequence, own_present.reshape(item_count))
    attended = attended.reshape(seq_dev, head_dev * head_size).astype(jnp.bfloat16)
    partial_out = jnp.dot(
        lax.all_gather(attended, "dp", axis=0, tiled=True),
        out_weight,
        preferred_element_type=jnp.float32,
    )
    return lax.psum_scatter(partial_out, "mp", scatter_dimension=0, tiled=True).astype(jnp.bfloat16)


def solution(mesh):
    placed = (
        P("dp", "mp", None),
        P("dp", None, "mp", None),
        P("dp", None, None, None, "mp", None),
        P("mp", None, None),
        P("mp", None, None),
        P(),
        P(),
        P("mp", "dp"),
    )
    return jax.shard_map(body, mesh=mesh, in_specs=placed, out_specs=P("mp", "dp"), check_vma=False)
```

profile of v0, /device:TPU:0, one launch (start us, length us, event | category | flops | bytes accessed | tf_op | source)
XLA Modules:
  0.0 179.9 jit_solution(16052660480834960542)
XLA Ops:
  6.6 0.8 copy.99
  8.9 32.8 %all_gather.6 = bf16[64,16,128]{2,1,0:T(8,128)(2,1)S(1)} all-gather(bf16[8,16,128]{2,1,0:T(8,128)(2,1)} %param.8), channel_id=1, replica_groups=mesh['dp'=8,'mp'=4] {'dp'}, dimensions={0}, use_global_device_ids=true | all-gather | bytes 294912 | tf_op jit(solution)/shard_map/all_gather | solution.py:114
  41.7 11.0 %copy.100 = bf16[1,8,8,128,2,128]{3,5,4,2,1,0:T(8,128)(2,1)} copy(bf16[1,8,8,128,2,128]{5,4,3,2,1,0:T(2,128)(2,1)} %param.10) | data formatting | bytes 8388608 | tf_op args[2]
  52.6 0.8 gather_fusion
  54.0 2.9 %fusion.6 = f32[2,128,64,128]{3,1,0,2:T(8,128)S(1)} fusion(bf16[64,128,2,128]{1,3,2,0:T(8,128)(2,1)} %bitcast.118, bf16[2,64,128]{2,1,0:T(8,128)(2,1)S(1)} %copy-done), kind=kOutput, calls=%fused_computation.8 | convolution fusion | flops 268435456 | bytes 10518528 | tf_op jit(solution)/shard_map/ptkr,krd->ptkd/dot_general | solution.py:32
  57.1 4.1 %fusion.89 = (f32[64,2,8]{2,1,0:T(2,128)S(1)}, f32[64,2,8,128]{3,2,1,0:T(8,128)S(1)}) fusion(f32[2,128,64,128]{3,1,0,2:T(8,128)S(1)} %fusion.6, bf16[64,16,128]{2,1,0:T(8,128)(2,1)S(1)} %gather_fusion.1, pred[64,128]{1,0:T(8,128)(4,1)S(1)} %fusion.69), kind=kOutput, calls=%fused_computation.106 | convolution fusion | flops 201718784 | bytes 9187328 | tf_op jit(solution)/shard_map/pkgd,ptkd->pkgt/dot_general | solution.py:38
  61.3 0.7 reshape.420
  61.9 5.6 %all-to-all-start = ((f32[8,1,128]{2,1,0:T(1,128)}), f32[8,1,128]{2,1,0:T(1,128)S(1)}, u32[]{:S(2)}, u32[]{:S(2)}) async-start(f32[8,1,128]{2,1,0:T(1,128)} %reshape.420), calls=%async_computation | async-start | bytes 8192 | tf_op jit(solution)/shard_map/all_to_all | solution.py:134
  68.1 2.1 %fusion.88 = (bf16[8,256,2,64]{3,2,1,0:T(2,128)(2,1)S(1)}, bf16[8,256,2,64]{3,2,1,0:T(2,128)(2,1)S(1)}) fusion(bf16[8,256,2,128]{3,2,1,0:T(2,128)(2,1)S(1)} %copy-done.3), kind=kLoop, calls=%fused_computation.105 | loop fusion | bytes 2097152 | tf_op jit(solution)/shard_map/slice | solution.py:34
  71.2 1.3 fusion.4
  72.5 14.0 %fusion = f32[64,2,8,128]{3,2,1,0:T(8,128)} fusion(f32[2,128,64,128]{3,1,0,2:T(8,128)S(1)} %fusion.4, f32[64,2,8,128]{3,2,1,0:T(8,128)S(1)} %get-tuple-element.14, f32[64,2,8]{2,1,0:T(2,128)S(1)} %get-tuple-element.13, pred[64,128]{1,0:T(8,128)(4,1)S(1)} %fusion.69), kind=kOutput, calls=%fused_computation.2 | convolution fusion | flops 201588736 | bytes 9449472 | tf_op jit(solution)/shard_map/pkgt,ptkd->pkgd/dot_general | solution.py:53
  87.0 1.1 fusion.90
  88.2 0.7 reshape.422
  88.9 6.0 %all-to-all-start.2 = ((f32[8,1,128]{2,1,0:T(1,128)}), f32[8,1,128]{2,1,0:T(1,128)S(1)}, u32[]{:S(2)}, u32[]{:S(2)}) async-start(f32[8,1,128]{2,1,0:T(1,128)} %reshape.422), calls=%async_computation.2 | async-start | bytes 8192 | tf_op jit(solution)/shard_map/all_to_all | solution.py:141
  95.2 6.3 %all-to-all-done.2 = f32[8,1,128]{2,1,0:T(1,128)S(1)} async-done(((f32[8,1,128]{2,1,0:T(1,128)}), f32[8,1,128]{2,1,0:T(1,128)S(1)}, u32[]{:S(2)}, u32[]{:S(2)}) %all-to-all-start.2) | async-done | bytes 4128 | tf_op jit(solution)/shard_map/all_to_all | solution.py:141
  101.5 3.5 %all-to-all-start.1 = ((f32[8,8,2,8,128]{4,3,2,1,0:T(8,128)}), f32[8,8,2,8,128]{4,3,2,1,0:T(8,128)S(1)}, u32[]{:S(2)}, u32[]{:S(2)}) async-start(f32[8,8,2,8,128]{4,3,2,1,0:T(8,128)} %bitcast.18), calls=%async_computation.1 | async-start | bytes 1048576 | tf_op jit(solution)/shard_map/all_to_all | solution.py:148
  105.7 0.7 reduce
  106.8 0.7 reduce.1
  108.0 7.5 %all-to-all-done.1 = f32[8,8,2,8,128]{4,3,2,1,0:T(8,128)S(1)} async-done(((f32[8,8,2,8,128]{4,3,2,1,0:T(8,128)}), f32[8,8,2,8,128]{4,3,2,1,0:T(8,128)S(1)}, u32[]{:S(2)}, u32[]{:S(2)}) %all-to-all-start.1) | async-done | bytes 524320 | tf_op jit(solution)/shard_map/all_to_all | solution.py:148
  115.9 1.9 %fusion.39 = bf16[1,8,16,128]{3,2,1,0:T(8,128)(2,1)S(1)} fusion(f32[2,128,8,256]{3,1,0,2:T(8,128)S(1)} %fusion.45, f32[8,2,8,256]{3,2,1,0:T(8,128)S(1)} %get-tuple-element.16, f32[8,2,8,128]{3,0,2,1:T(8,128)S(1)} %fusion.49, f32[8,2,8]{2,1,0:T(2,128)S(1)} %get-tuple-element.15, pred[8,256]{1,0:T(8,128)(4,1)S(1)} %iota_compare_fusion.2, ...), kind=kOutput, calls=%fused_computation.23 | convolution fusion | flops 50462720 | bytes 2330112 | tf_op jit(solution)/shard_map/pkgt,ptkd->pkgd/dot_general | solution.py:53
  117.8 30.7 %all_gather.7 = bf16[64,2048]{1,0:T(8,128)(2,1)S(1)} all-gather(bf16[8,2048]{1,0:T(8,128)(2,1)S(1)} %bitcast.126), channel_id=1, replica_groups=mesh['dp'=8,'mp'=4] {'dp'}, dimensions={0}, use_global_device_ids=true | all-gather | bytes 294912 | tf_op jit(solution)/shard_map/all_gather | solution.py:164
  148.6 3.7 %fusion.91 = f32[64,1024]{1,0:T(8,128)} fusion(bf16[64,2048]{1,0:T(8,128)(2,1)S(1)} %all_gather.7, bf16[2048,1024]{1,0:T(8,128)(2,1)} %param.15), kind=kOutput, calls=%fused_computation.108 | convolution fusion | flops 268435456 | bytes 4718592 | tf_op jit(solution)/shard_map/dot_general | solution.py:163
  152.3 19.2 %reduce-scatter.2.cloned.1.call-done = f32[16,1024]{1,0:T(8,128)} async-done(((f32[64,1024]{1,0:T(8,128)}), f32[16,1024]{1,0:T(8,128)}) %reduce-scatter.2.cloned.1.call-update) | async-done | bytes 65552 | tf_op jit(solution)/shard_map/reduce_scatter | solution.py:168
  171.6 1.5 convert_element_type.18
  (73 shorter events, 6.9 us)
Async XLA Ops:
  6.5 47.5 %copy-start = (bf16[2,64,128]{2,1,0:T(8,128)(2,1)S(1)}, bf16[2,64,128]{2,1,0:T(8,128)(2,1)}, u32[]{:S(2)}) copy-start(bf16[2,64,128]{2,1,0:T(8,128)(2,1)} %param.11) | copy-start | bytes 98308
  41.7 11.0 %copy-start.1 = (s32[64]{0:T(128)S(1)}, s32[64]{0:T(128)}, u32[]{:S(2)}) copy-start(s32[64]{0:T(128)} %param.13) | copy-start | bytes 772
  57.0 11.1 %copy-start.3 = (bf16[8,256,2,128]{3,2,1,0:T(2,128)(2,1)S(1)}, bf16[8,256,2,128]{3,2,1,0:T(2,128)(2,1)}, u32[]{:S(2)}) copy-start(bf16[8,256,2,128]{3,2,1,0:T(2,128)(2,1)} %param.9) | copy-start | bytes 3145732
  61.2 10.0 %copy-start.4 = (bf16[2,64,128]{2,1,0:T(8,128)(2,1)S(1)}, bf16[2,64,128]{2,1,0:T(8,128)(2,1)}, u32[]{:S(2)}) copy-start(bf16[2,64,128]{2,1,0:T(8,128)(2,1)} %param.12) | copy-start | bytes 98308
  61.9 26.9 %all-to-all-start = ((f32[8,1,128]{2,1,0:T(1,128)}), f32[8,1,128]{2,1,0:T(1,128)S(1)}, u32[]{:S(2)}, u32[]{:S(2)}) async-start(f32[8,1,128]{2,1,0:T(1,128)} %reshape.420), calls=%async_computation | async-start | bytes 8192 | tf_op jit(solution)/shard_map/all_to_all | solution.py:134
  68.0 3.2 %copy-start.2 = (bf16[1,8,8,128,2,128]{3,5,4,2,1,0:T(8,128)(2,1)S(1)}, bf16[1,8,8,128,2,128]{3,5,4,2,1,0:T(8,128)(2,1)}, u32[]{:S(2)}) copy-start(bf16[1,8,8,128,2,128]{3,5,4,2,1,0:T(8,128)(2,1)} %copy.100) | copy-start | bytes 12582916
  72.5 14.5 %copy-start.5 = (bf16[8,16,128]{2,1,0:T(8,128)(2,1)S(1)}, bf16[8,16,128]{2,1,0:T(8,128)(2,1)}, u32[]{:S(2)}) copy-start(bf16[8,16,128]{2,1,0:T(8,128)(2,1)} %param.8) | copy-start | bytes 98308
  88.9 12.6 %all-to-all-start.2 = ((f32[8,1,128]{2,1,0:T(1,128)}), f32[8,1,128]{2,1,0:T(1,128)S(1)}, u32[]{:S(2)}, u32[]{:S(2)}) async-start(f32[8,1,128]{2,1,0:T(1,128)} %reshape.422), calls=%async_computation.2 | async-start | bytes 8192 | tf_op jit(solution)/shard_map/all_to_all | solution.py:141
  101.5 14.1 %all-to-all-start.1 = ((f32[8,8,2,8,128]{4,3,2,1,0:T(8,128)}), f32[8,8,2,8,128]{4,3,2,1,0:T(8,128)S(1)}, u32[]{:S(2)}, u32[]{:S(2)}) async-start(f32[8,8,2,8,128]{4,3,2,1,0:T(8,128)} %bitcast.18), calls=%async_computation.1 | async-start | bytes 1048576 | tf_op jit(solution)/shard_map/all_to_all | solution.py:148
  105.0 66.6 %reduce-scatter.2.cloned.1.call-start = ((), (), s32[]{:S(2)}) async-start(), calls=%async_computation.4 | async-start | bytes 327680 | tf_op jit(solution)/shard_map/reduce_scatter | solution.py:168
Sparse Core Ops, SparseCore 0:
  152.5 19.0 reduce-scatter.1
where the time goes:
time: 181 us; the launch traced here: 180 us
  blocking collectives  63.5 us (35%)
  waiting for transfers between devices  33 us (18%)
  matrix products  30.6 us (17%)
  local copies, waits for them, and re-layouts  18.9 us (10%)
  starting transfers between devices  15.1 us (8%)
  between operations  13.7 us (8%)
  other arithmetic  5.04 us (3%)
    all_gather x1, blocking collectives, body(): all_queries = lax.all_gather(queries, 'dp', axis=0, tiled=True)  32.8 us
    all_gather x1, blocking collectives, body(): lax.all_gather(attended, 'dp', axis=0, tiled=True)  30.7 us
    reduce_scatter x1, waiting for transfers between devices, body(): lax.psum_scatter(partial_out, 'mp', scatter_dimension=0, tiled=True)  19.2 us
    dot_general x2, matrix products, page_partials(): jnp.einsum('pkgt,ptkd->pkgd', weights, rebuilt_values, precision=highest)  15.8 us
    unnamed x19, local copies, waits for them, and re-layouts  13.3 us
    all_to_all x1, waiting for transfers between devices, body(): lax.all_to_all(weighted.reshape(group_count, slot_count, kv_heads, head_c...  7.5 us
    all_to_all x1, waiting for transfers between devices, body(): lax.all_to_all(weight_sum.reshape(group_count, slot_count, kv_heads, head...  6.28 us
    all_to_all x1, starting transfers between devices, body(): lax.all_to_all(weight_sum.reshape(group_count, slot_count, kv_heads, head...  6 us
  transfers between devices with their start and end apart: 4, of which 3 were waited for; matrix products, arithmetic and copies ran while one was open for 14% of the time, Pallas kernels for 0%

commit v1 on v0

v1 whole, which is shorter than its diff:
```python
import math

import jax
import jax.numpy as jnp
from jax import lax
from jax.experimental import pallas as pl
from jax.experimental.pallas import tpu as pltpu
from jax.sharding import PartitionSpec as P

very_low = -1e30
f32 = jnp.float32
bf16 = jnp.bfloat16
lanes = 128
half = 64
pad_heads = 16
stat_lanes = 16


def three_terms(value):
    high = value.astype(bf16)
    rest = value - high.astype(f32)
    middle = rest.astype(bf16)
    low = (rest - middle.astype(f32)).astype(bf16)
    return high, middle, low


def absorbed_queries(query_rows, key_up, kv_heads):
    scale = math.log2(math.e) / math.sqrt(key_up.shape[1])
    product = lax.dot_general(
        query_rows, key_up, (((1,), (1,)), ((), ())), preferred_element_type=f32
    )
    lane = lax.broadcasted_iota(jnp.int32, (1, 1, lanes), 2)
    if kv_heads == 2:
        product = product.reshape(-1, 2, 8, lanes)
        first = product[:, 0]
        second = pltpu.roll(product[:, 1].reshape(-1, lanes), half, 1).reshape(first.shape)
    else:
        product = jnp.concatenate([product, jnp.zeros_like(product)], axis=1)
        first = product.reshape(-1, 8, lanes)
        second = jnp.zeros_like(first)
    both = jnp.concatenate([first, second], axis=1)
    both = jnp.where(lane < half, both * scale, 0.0)
    return jnp.concatenate(three_terms(both), axis=1)


def attend(query_terms, latent, valid):
    scores = lax.dot_general(
        query_terms, latent, (((1,), (1,)), ((), ())), preferred_element_type=f32
    )
    scores = scores[0:16] + scores[16:32] + scores[32:48]
    scores = jnp.where(valid, scores, very_low)
    peak = jnp.max(scores, axis=1, keepdims=True)
    weights = jnp.exp2(scores - peak)
    total = jnp.sum(weights, axis=1, keepdims=True)
    high = weights.astype(bf16)
    low = (weights - high.astype(f32)).astype(bf16)
    weighted = jnp.dot(
        jnp.concatenate([high, low], axis=0), latent, preferred_element_type=f32
    )
    weighted = (weighted[0:16] + weighted[16:32]) / total
    lane = lax.broadcasted_iota(jnp.int32, (8, lanes), 1)
    packed = jnp.where(lane < half, pltpu.roll(weighted[0:8], half, 1), weighted[8:16])
    return packed, peak + jnp.log2(total)


def row_masks(rows, kv_heads):
    column = lax.broadcasted_iota(jnp.int32, (pad_heads, rows), 1)
    head = lax.broadcasted_iota(jnp.int32, (pad_heads, rows), 0) // 8
    if kv_heads == 1:
        return column, head == 0
    return column // 2, (column % 2) == head


def solution(mesh):
    group_count = mesh.shape["dp"]
    head_parts = mesh.shape["mp"]

    def home_kernel(
        routes, lengths, own, queries, key_up, resident,
        item_sequence, item_tokens, entry_item, entry_ok, packed_out, lse_out,
        table, counts, holder_counts,
    ):
        seq_dev, rows, _ = resident.shape
        kv_heads = key_up.shape[0] // half
        items = item_sequence.shape[0]
        slots = items // group_count
        entry_count = routes.shape[0] // group_count
        tail_pages = entry_count // seq_dev
        home_tokens = rows // kv_heads
        page = lanes
        me = own[0]

        def scan_group(group, _):
            count = jnp.int32(0)
            for entry in range(entry_count):
                table[group * slots + count] = entry
                count = count + (routes[group * entry_count + entry] == me).astype(jnp.int32)
            counts[group] = count
            return 0

        lax.fori_loop(0, group_count, scan_group, 0)

        def finish_item(group, _):
            for slot in range(slots):
                here = slot < counts[group]
                entry = jnp.where(here, table[group * slots + slot], 0)
                row = entry // tail_pages
                sequence = group * seq_dev + row
                first = home_tokens + (entry - row * tail_pages) * page
                count = jnp.clip(lengths[sequence] - first, 0, page)
                item_sequence[group * slots + slot] = sequence
                item_tokens[group * slots + slot] = jnp.where(here, count, 0)
            return 0

        lax.fori_loop(0, group_count, finish_item, 0)

        def clear(holder, _):
            holder_counts[holder] = 0
            return 0

        lax.fori_loop(0, group_count, clear, 0)

        def own_row(row, _):
            length = lengths[me * seq_dev + row]
            for page_index in range(tail_pages):
                entry = row * tail_pages + page_index
                holder = routes[me * entry_count + entry]
                slot = holder_counts[holder]
                holder_counts[holder] = slot + 1
                entry_item[entry] = holder * slots + slot
                entry_ok[entry] = (home_tokens + page_index * page < length).astype(jnp.int32)
            return 0

        lax.fori_loop(0, seq_dev, own_row, 0)

        terms = absorbed_queries(queries[...], key_up[...], kv_heads)
        token, head_ok = row_masks(rows, kv_heads)
        for row in range(seq_dev):
            valid = head_ok & (token < lengths[me * seq_dev + row])
            packed, lse = attend(terms[row], resident[row], valid)
            packed_out[row] = packed
            lse_out[row] = jnp.broadcast_to(lse, (pad_heads, lanes))

    def page_kernel(
        item_sequence, item_tokens, queries, key_up, overflow, out, pages, terms_ref, sems
    ):
        items, rows, _ = overflow.shape
        slots = items // group_count
        kv_heads = key_up.shape[0] // half

        def copy_of(group):
            part = pl.ds(group * slots, slots)
            return pltpu.make_async_copy(overflow.at[part], pages.at[part], sems.at[group])

        for group in range(group_count):
            copy_of(group).start()
        terms_ref[...] = absorbed_queries(queries[...], key_up[...], kv_heads)
        token, head_ok = row_masks(rows, kv_heads)
        stat_lane = lax.broadcasted_iota(jnp.int32, (pad_heads, lanes), 1)

        def one_group(group, _):
            copy_of(group).wait()
            stats = jnp.zeros((pad_heads, lanes), f32)
            for slot in range(slots):
                item = group * slots + slot
                valid = head_ok & (token < item_tokens[item])
                packed, lse = attend(terms_ref[item_sequence[item]], pages[item], valid)
                out[group, slot] = packed.astype(bf16)
                for place, term in enumerate(three_terms(lse)):
                    chosen = stat_lane == slot * stat_lanes + place
                    stats = jnp.where(chosen, term.astype(f32), stats)
            out[group, slots] = stats[0:8].astype(bf16)
            out[group, slots + 1] = stats[8:16].astype(bf16)
            return 0

        lax.fori_loop(0, group_count, one_group, 0)

    def merge_kernel(entry_item, entry_ok, received, packed_home, lse_home, out, rows_ref):
        seq_dev = packed_home.shape[0]
        slots = received.shape[1] - 2
        tail_pages = entry_item.shape[0] // seq_dev
        lane8 = lax.broadcasted_iota(jnp.int32, (8, lanes), 1)
        lane16 = lax.broadcasted_iota(jnp.int32, (pad_heads, lanes), 1)
        is_term = (lane16 % stat_lanes) < 3
        slot_of_lane = lane16 // stat_lanes

        def spread(value):
            return jnp.where(lane8 < half, value[0:8], value[8:16])

        for row in range(seq_dev):
            parts = [(lse_home[row], packed_home[row])]
            for page_index in range(tail_pages):
                entry = row * tail_pages + page_index
                item = entry_item[entry]
                holder = item // slots
                slot = item - holder * slots
                stats = jnp.concatenate(
                    [received[holder, slots].astype(f32), received[holder, slots + 1].astype(f32)],
                    axis=0,
                )
                mine = is_term & (slot_of_lane == slot)
                lse = jnp.sum(jnp.where(mine, stats, 0.0), axis=1, keepdims=True)
                lse = jnp.where(entry_ok[entry] > 0, lse, very_low)
                lse = jnp.broadcast_to(lse, (pad_heads, lanes))
                parts.append((lse, received[holder, slot].astype(f32)))
            peak = parts[0][0]
            for lse, _ in parts[1:]:
                peak = jnp.maximum(peak, lse)
            total = jnp.zeros((8, lanes), f32)
            merged = jnp.zeros((8, lanes), f32)
            for lse, packed in parts:
                factor = spread(jnp.exp2(lse - peak))
                total = total + factor
                merged = merged + factor * packed
            rows_ref[row * 8 : (row + 1) * 8, :] = merged / total
        for query in range(8):
            block = rows_ref[pl.ds(query, seq_dev, stride=8), :].astype(bf16)
            for target in range(group_count):
                out[target, query] = block

    def project_kernel(received, value_up, weight, out):
        sequences = received.shape[0] * received.shape[2]
        kv_heads = value_up.shape[1] // lanes
        pieces = [
            jnp.dot(
                received[:, query].astype(f32).reshape(sequences, lanes).astype(bf16),
                value_up[...],
                preferred_element_type=f32,
            ).astype(bf16)
            for query in range(8)
        ]
        attended = jnp.concatenate(
            [
                piece[:, head * lanes : (head + 1) * lanes]
                for head in range(kv_heads)
                for piece in pieces
            ],
            axis=1,
        )
        result = jnp.dot(attended, weight[...], preferred_element_type=f32)
        out[...] = result.astype(bf16)

    def body(
        queries, resident_cache, overflow_cache, key_up_weight, value_up_weight,
        lengths, routes, out_weight,
    ):
        seq_dev, head_dev, head_size = queries.shape
        kv_heads, width, _ = key_up_weight.shape
        slots = overflow_cache.shape[2]
        page = overflow_cache.shape[3]
        items = group_count * slots
        tail_pages = routes.shape[1]
        home_tokens = resident_cache.shape[1]
        smem = pl.BlockSpec(memory_space=pltpu.SMEM)
        vmem = pl.BlockSpec(memory_space=pltpu.VMEM)
        hbm = pl.BlockSpec(memory_space=pl.ANY)
        ints = lambda size: jax.ShapeDtypeStruct((size,), jnp.int32)
        own = lax.axis_index("dp").astype(jnp.int32).reshape(1)
        flat_routes = routes.reshape(-1)
        key_up = key_up_weight.reshape(kv_heads * width, head_size)
        flat_queries = queries.reshape(seq_dev * head_dev, head_size)

        spread_queries = jnp.broadcast_to(
            flat_queries[None], (group_count,) + flat_queries.shape
        )
        all_queries = lax.all_to_all(
            spread_queries, "dp", split_axis=0, concat_axis=0, tiled=True
        ).reshape(-1, head_size)

        entries = seq_dev * tail_pages
        item_sequence, item_tokens, entry_item, entry_ok, packed_home, lse_home = pl.pallas_call(
            home_kernel,
            out_shape=(
                ints(items), ints(items), ints(entries), ints(entries),
                jax.ShapeDtypeStruct((seq_dev, 8, lanes), f32),
                jax.ShapeDtypeStruct((seq_dev, pad_heads, lanes), f32),
            ),
            in_specs=[smem, smem, smem, vmem, vmem, vmem],
            out_specs=(smem, smem, smem, smem, vmem, vmem),
            scratch_shapes=[
                pltpu.SMEM((items + 8,), jnp.int32),
                pltpu.SMEM((group_count,), jnp.int32),
                pltpu.SMEM((group_count,), jnp.int32),
            ],
            cost_estimate=pl.CostEstimate(
                flops=200_000_000, transcendentals=0, bytes_accessed=1 << 20
            ),
        )(
            flat_routes, lengths, own, flat_queries, key_up,
            resident_cache.reshape(seq_dev, home_tokens * kv_heads, lanes),
        )

        partials = pl.pallas_call(
            page_kernel,
            out_shape=jax.ShapeDtypeStruct((group_count, slots + 2, 8, lanes), bf16),
            in_specs=[smem, smem, vmem, vmem, hbm],
            out_specs=vmem,
            scratch_shapes=[
                pltpu.VMEM((items, page * kv_heads, lanes), bf16),
                pltpu.VMEM((group_count * seq_dev, 48, lanes), bf16),
                pltpu.SemaphoreType.DMA((group_count,)),
            ],
        )(
            item_sequence, item_tokens, all_queries, key_up,
            overflow_cache.reshape(items, page * kv_heads, lanes),
        )
        partials = lax.all_to_all(partials, "dp", split_axis=0, concat_axis=0, tiled=True)

        merged = pl.pallas_call(
            merge_kernel,
            out_shape=jax.ShapeDtypeStruct((group_count, 8, seq_dev, lanes), bf16),
            in_specs=[smem, smem, vmem, vmem, vmem],
            out_specs=vmem,
            scratch_shapes=[pltpu.VMEM((seq_dev * 8, lanes), f32)],
        )(entry_item, entry_ok, partials, packed_home, lse_home)
        merged = lax.all_to_all(merged, "dp", split_axis=0, concat_axis=0, tiled=True)

        blocks = jnp.eye(kv_heads, dtype=bf16)[:, None, :, None] * value_up_weight[:, :, None, :]
        blocks = blocks.reshape(kv_heads * width, kv_heads * head_size)
        blocks = jnp.pad(blocks, ((0, lanes - kv_heads * width), (0, 0)))
        sequences = group_count * seq_dev
        partial_out = pl.pallas_call(
            project_kernel,
            out_shape=jax.ShapeDtypeStruct((sequences, out_weight.shape[1]), bf16),
            in_specs=[vmem, vmem, vmem],
            out_specs=vmem,
        )(merged, blocks, out_weight)
        pieces = lax.all_to_all(
            partial_out.reshape(head_parts, sequences // head_parts, -1),
            "mp", split_axis=0, concat_axis=0, tiled=True,
        )
        return jnp.sum(pieces.astype(f32), axis=0).astype(bf16)

    placed = (
        P("dp", "mp", None),
        P("dp", None, "mp", None),
        P("dp", None, None, None, "mp", None),
        P("mp", None, None),
        P("mp", None, None),
        P(),
        P(),
        P("mp", "dp"),
    )
    return jax.shard_map(body, mesh=mesh, in_specs=placed, out_specs=P("mp", "dp"), check_vma=False)
```

time: 181 us -> 78.4 us (0.43)
  blocking collectives: 63.5 us -> 20.6 us
  Pallas kernels: 0 us -> 33.2 us
  matrix products: 30.6 us -> 0 us
  waiting for transfers between devices: 33 us -> 7.5 us
  local copies, waits for them, and re-layouts: 18.9 us -> 4.95 us
  between operations: 13.7 us -> 0.05 us
  starting transfers between devices: 15.1 us -> 10.7 us
  other arithmetic: 5.04 us -> 0.76 us
    all_gather x2 -> x0, blocking collectives: 63.5 us -> none  [the longest x1 32.8 us: body(): all_queries = lax.all_gather(queries, 'dp', axis=0, tiled=True)]
    pallas_call x0 -> x4, Pallas kernels: none -> 33.2 us  [the longest x1 20.7 us: body(): pl.pallas_call(page_kernel, out_shape=jax.ShapeDtypeStruct((group_count,...]
    dot_general x11 -> x0, matrix products: 30.5 us -> none  [the longest x2 15.8 us: page_partials(): jnp.einsum('pkgt,ptkd->pkgd', weights, rebuilt_values, precision=highest)]
    all_to_all x0 -> x2, blocking collectives: none -> 20.6 us  [the longest x1 12.7 us: body(): lax.all_to_all(partials, 'dp', split_axis=0, concat_axis=0, tiled=True)]
    reduce_scatter x1 -> x0, waiting for transfers between devices: 19.2 us -> none  [body(): lax.psum_scatter(partial_out, 'mp', scatter_dimension=0, tiled=True)]
    unnamed x19 -> x8, local copies, waits for them, and re-layouts: 13.3 us -> 2.75 us
    all_to_all x3 -> x2, waiting for transfers between devices: 13.8 us -> 7.5 us  [the longest x1 6.5 us: body(): lax.all_to_all(merged, 'dp', split_axis=0, concat_axis=0, tiled=True)]
    all_to_all x3 -> x2, starting transfers between devices: 15.1 us -> 10.7 us  [the longest x1 7.31 us: body(): lax.all_to_all(spread_queries, 'dp', split_axis=0, concat_axis=0, tiled=T...]
  transfers between devices with their start and end apart: 4 -> 2, of which waited for: 3 -> 2; matrix products, arithmetic and copies ran while one was open for 14% -> 3% of each run, Pallas kernels for 0% -> 8%
where the time goes in v1:
time: 78.4 us; the launch traced here: 77.7 us
  Pallas kernels  33.2 us (42%)
  blocking collectives  20.6 us (26%)
  starting transfers between devices  10.7 us (14%)
  waiting for transfers between devices  7.5 us (10%)
  local copies, waits for them, and re-layouts  4.95 us (6%)
    pallas_call x1, Pallas kernels, body(): pl.pallas_call(page_kernel, out_shape=jax.ShapeDtypeStruct((group_count,...  20.7 us
    all_to_all x1, blocking collectives, body(): lax.all_to_all(partials, 'dp', split_axis=0, concat_axis=0, tiled=True)  12.7 us
    all_to_all x1, blocking collectives, body(): lax.all_to_all(partial_out.reshape(head_parts, sequences // head_parts, -...  7.89 us
    all_to_all x1, starting transfers between devices, body(): lax.all_to_all(spread_queries, 'dp', split_axis=0, concat_axis=0, tiled=T...  7.31 us
    all_to_all x1, waiting for transfers between devices, body(): lax.all_to_all(merged, 'dp', split_axis=0, concat_axis=0, tiled=True)  6.5 us
    pallas_call x1, Pallas kernels, body(): pl.pallas_call(home_kernel, out_shape=(ints(items), ints(items), ints(ent...  6.44 us
    pallas_call x1, Pallas kernels, body(): pl.pallas_call(project_kernel, out_shape=jax.ShapeDtypeStruct((sequences,...  3.91 us
    all_to_all x1, starting transfers between devices, body(): lax.all_to_all(merged, 'dp', split_axis=0, concat_axis=0, tiled=True)  3.37 us
  transfers between devices with their start and end apart: 2, of which 2 were waited for; matrix products, arithmetic and copies ran while one was open for 3% of the time, Pallas kernels for 8%

profile of v1, /device:TPU:0, one launch (start us, length us, event | category | flops | bytes accessed | tf_op | source)
XLA Modules:
  0.0 77.7 jit_solution(17396065041399868040)
XLA Ops:
  0.0 0.0 copy-start.2
  0.0 1.5 %broadcast_in_dim.2 = bf16[8,128,128]{2,1,0:T(8,128)(2,1)} broadcast(bf16[128,128]{1,0:T(8,128)(2,1)} %bitcast.22), dimensions={1,2} | broadcast | bytes 294912 | tf_op jit(solution)/shard_map/broadcast_in_dim | solution.py:263
  1.5 7.3 %all-to-all-start = ((bf16[8,128,128]{2,1,0:T(8,128)(2,1)}), bf16[8,128,128]{2,1,0:T(8,128)(2,1)S(1)}, u32[]{:S(2)}, u32[]{:S(2)}) async-start(bf16[8,128,128]{2,1,0:T(8,128)(2,1)} %broadcast_in_dim.2), calls=%async_computation | async-start | bytes 524288 | tf_op jit(solution)/shard_map/all_to_all | solution.py:266
  8.8 0.8 copy.9
  9.6 0.7 reshape.38.routes
  10.3 6.4 %shard_map.82 = (s32[64]{0:T(128)}, s32[64]{0:T(128)}, s32[48]{0:T(128)}, s32[48]{0:T(128)}, f32[8,8,128]{2,1,0:T(8,128)}, /*index=5*/f32[8,16,128]{2,1,0:T(8,128)}) custom-call(s32[384]{0:T(512)} %reshape.38.routes, s32[64]{0:T(128)} %lengths.1, s32[1]{0:T(128)} %bitcast.own, bf16[128,128]{1,0:T(8,128)(2,1)} %bitcast.23, bf16[128,128]{1,0:T(8,128)(2,1)} %bitcast.20, ...), custom_call_target="tpu_custom_call" | custom-call | flops 200000000 | bytes 1048576 | tf_op jit(solution)/shard_map/pallas_call | solution.py:271
  16.7 1.0 %all-to-all-done = bf16[8,128,128]{2,1,0:T(8,128)(2,1)S(1)} async-done(((bf16[8,128,128]{2,1,0:T(8,128)(2,1)}), bf16[8,128,128]{2,1,0:T(8,128)(2,1)S(1)}, u32[]{:S(2)}, u32[]{:S(2)}) %all-to-all-start) | async-done | bytes 262176 | tf_op jit(solution)/shard_map/all_to_all | solution.py:266
  17.7 0.0 copy-start
  17.7 0.7 copy-done
  18.4 20.7 %shard_map.83 = bf16[8,10,8,128]{3,2,1,0:T(8,128)(2,1)} custom-call(s32[64]{0:T(128)} %get-tuple-element.13.item_sequence, s32[64]{0:T(128)} %get-tuple-element.14.item_tokens, bf16[1024,128]{1,0:T(8,128)(2,1)} %bitcast.16, bf16[128,128]{1,0:T(8,128)(2,1)} %bitcast.21, bf16[64,256,128]{2,1,0:T(8,128)(2,1)} %bitcast.14), custom_call_target="tpu_custom_call" | custom-call | tf_op jit(solution)/shard_map/pallas_call | solution.py:293
  39.2 12.7 %all_to_all.20.received = bf16[8,10,8,128]{3,2,1,0:T(8,128)(2,1)} all-to-all(bf16[8,10,8,128]{3,2,1,0:T(8,128)(2,1)} %shard_map.83), channel_id=1, replica_groups=mesh['dp'=8,'mp'=4] {'dp'}, dimensions={0} | all-to-all | bytes 327680 | tf_op jit(solution)/shard_map/all_to_all | solution.py:307
  51.8 2.1 %shard_map.84 = bf16[8,8,8,128]{3,2,1,0:T(8,128)(2,1)} custom-call(s32[48]{0:T(128)} %get-tuple-element.11.entry_item, s32[48]{0:T(128)} %get-tuple-element.12.entry_ok, bf16[8,10,8,128]{3,2,1,0:T(8,128)(2,1)} %all_to_all.20.received, f32[8,8,128]{2,1,0:T(8,128)} %get-tuple-element.15.packed_home, f32[8,16,128]{2,1,0:T(8,128)} %get-tuple-element.16.lse_home), custom_call_target="tpu_custom_call" | custom-call | tf_op jit(solution)/shard_map/pallas_call | solution.py:309
  53.9 3.4 %all-to-all-start.2 = ((bf16[8,8,8,128]{3,2,1,0:T(8,128)(2,1)}), bf16[8,8,8,128]{3,2,1,0:T(8,128)(2,1)S(1)}, u32[]{:S(2)}, u32[]{:S(2)}) async-start(bf16[8,8,8,128]{3,2,1,0:T(8,128)(2,1)} %shard_map.84), calls=%async_computation.2 | async-start | bytes 262144 | tf_op jit(solution)/shard_map/all_to_all | solution.py:316
  57.3 0.0 copy-done.2
  57.3 0.1 broadcast_multiply_fusion
  57.5 0.6 copy.12
  58.1 6.5 %all-to-all-done.2.received = bf16[8,8,8,128]{3,2,1,0:T(8,128)(2,1)S(1)} async-done(((bf16[8,8,8,128]{3,2,1,0:T(8,128)(2,1)}), bf16[8,8,8,128]{3,2,1,0:T(8,128)(2,1)S(1)}, u32[]{:S(2)}, u32[]{:S(2)}) %all-to-all-start.2) | async-done | bytes 131104 | tf_op jit(solution)/shard_map/all_to_all | solution.py:316
  64.6 0.0 copy-start.1
  64.6 0.6 copy-done.1
  65.2 3.9 %shard_map.85 = bf16[64,1024]{1,0:T(8,128)(2,1)} custom-call(bf16[8,8,8,128]{3,2,1,0:T(8,128)(2,1)} %copy-done.1, bf16[128,256]{1,0:T(8,128)(2,1)} %bitcast.18, bf16[2048,1024]{1,0:T(8,128)(2,1)} %weight.1), custom_call_target="tpu_custom_call" | custom-call | tf_op jit(solution)/shard_map/pallas_call | solution.py:322
  69.1 7.9 %all_to_all.21 = bf16[4,16,1024]{2,1,0:T(8,128)(2,1)S(1)} all-to-all(bf16[4,16,1024]{2,1,0:T(8,128)(2,1)} %bitcast.17), channel_id=1, replica_groups=mesh['dp'=8,'mp'=4] {'mp'}, dimensions={0} | all-to-all | bytes 262144 | tf_op jit(solution)/shard_map/all_to_all | solution.py:328
  77.0 0.6 reduce_sum.12
  (1 shorter events, 0.0 us)
Async XLA Ops:
  0.0 57.3 %copy-start.2 = (bf16[2,64,128]{2,1,0:T(8,128)(2,1)S(1)}, bf16[2,64,128]{2,1,0:T(8,128)(2,1)}, u32[]{:S(2)}) copy-start(bf16[2,64,128]{2,1,0:T(8,128)(2,1)} %param.12) | copy-start | bytes 98308
  1.5 16.2 %all-to-all-start = ((bf16[8,128,128]{2,1,0:T(8,128)(2,1)}), bf16[8,128,128]{2,1,0:T(8,128)(2,1)S(1)}, u32[]{:S(2)}, u32[]{:S(2)}) async-start(bf16[8,128,128]{2,1,0:T(8,128)(2,1)} %broadcast_in_dim.2), calls=%async_computation | async-start | bytes 524288 | tf_op jit(solution)/shard_map/all_to_all | solution.py:266
  17.7 0.7 copy-start
  53.9 10.7 %all-to-all-start.2 = ((bf16[8,8,8,128]{3,2,1,0:T(8,128)(2,1)}), bf16[8,8,8,128]{3,2,1,0:T(8,128)(2,1)S(1)}, u32[]{:S(2)}, u32[]{:S(2)}) async-start(bf16[8,8,8,128]{3,2,1,0:T(8,128)(2,1)} %shard_map.84), calls=%async_computation.2 | async-start | bytes 262144 | tf_op jit(solution)/shard_map/all_to_all | solution.py:316
  64.6 0.6 copy-start.1

commit v2 on v1

v2 whole, which is shorter than its diff:
```python
import math

import jax
import jax.numpy as jnp
from jax import lax
from jax.experimental import pallas as pl
from jax.experimental.pallas import tpu as pltpu
from jax.sharding import PartitionSpec as P

very_low = -1e30
f32 = jnp.float32
bf16 = jnp.bfloat16
lanes = 128
half = 64
pad_heads = 16
stat_lanes = 16
batch = 8


def three_terms(value):
    high = value.astype(bf16)
    rest = value - high.astype(f32)
    middle = rest.astype(bf16)
    low = (rest - middle.astype(f32)).astype(bf16)
    return high, middle, low


def absorbed_queries(query_rows, key_up, kv_heads):
    scale = math.log2(math.e) / math.sqrt(key_up.shape[1])
    product = lax.dot_general(
        query_rows, key_up, (((1,), (1,)), ((), ())), preferred_element_type=f32
    )
    lane = lax.broadcasted_iota(jnp.int32, (1, 1, lanes), 2)
    if kv_heads == 2:
        product = product.reshape(-1, 2, 8, lanes)
        first = product[:, 0]
        second = pltpu.roll(product[:, 1].reshape(-1, lanes), half, 1).reshape(first.shape)
    else:
        product = jnp.concatenate([product, jnp.zeros_like(product)], axis=1)
        first = product.reshape(-1, 8, lanes)
        second = jnp.zeros_like(first)
    both = jnp.concatenate([first, second], axis=1)
    both = jnp.where(lane < half, both * scale, 0.0)
    return jnp.concatenate(three_terms(both), axis=1)


def attend_all(query_terms, latents, valid):
    products = [
        lax.dot_general(terms, latent, (((1,), (1,)), ((), ())), preferred_element_type=f32)
        for terms, latent in zip(query_terms, latents)
    ]
    scores = [
        jnp.where(ok, product[0:16] + product[16:32] + product[32:48], very_low)
        for ok, product in zip(valid, products)
    ]
    peaks = [jnp.max(score, axis=1, keepdims=True) for score in scores]
    weights = [jnp.exp2(score - peak) for score, peak in zip(scores, peaks)]
    split = []
    for weight in weights:
        high = weight.astype(bf16)
        low = (weight - high.astype(f32)).astype(bf16)
        split.append(jnp.concatenate([high, low], axis=0))
    sums = [
        jnp.dot(terms, latent, preferred_element_type=f32)
        for terms, latent in zip(split, latents)
    ]
    totals = [jnp.sum(weight, axis=1, keepdims=True) for weight in weights]
    lane = lax.broadcasted_iota(jnp.int32, (8, lanes), 1)
    packed = []
    for weighted, total in zip(sums, totals):
        weighted = (weighted[0:16] + weighted[16:32]) / total
        packed.append(
            jnp.where(lane < half, pltpu.roll(weighted[0:8], half, 1), weighted[8:16])
        )
    return packed, [peak + jnp.log2(total) for peak, total in zip(peaks, totals)]


def row_masks(rows, kv_heads):
    column = lax.broadcasted_iota(jnp.int32, (pad_heads, rows), 1)
    head = lax.broadcasted_iota(jnp.int32, (pad_heads, rows), 0) // 8
    if kv_heads == 1:
        return column, head == 0
    return column // 2, (column % 2) == head


def pin(array):
    return pltpu.with_memory_space_constraint(array, pltpu.VMEM)


def near(shape, kind):
    return pltpu.VMEM(shape, kind)


def solution(mesh):
    group_count = mesh.shape["dp"]
    head_parts = mesh.shape["mp"]

    def home_kernel(
        routes, lengths, own, queries, key_up, resident,
        item_sequence, item_tokens, item_list, item_count, entry_item, entry_ok,
        packed_out, lse_out, table, counts, holder_counts,
    ):
        seq_dev, rows, _ = resident.shape
        kv_heads = key_up.shape[0] // half
        items = item_sequence.shape[0]
        slots = items // group_count
        tail_pages = routes.shape[0]
        home_tokens = rows // kv_heads
        page = lanes
        me = own[0]

        def scan_group(group, _):
            count = jnp.int32(0)
            for row in range(seq_dev):
                for place in range(tail_pages):
                    table[group * slots + count] = row * tail_pages + place
                    named = routes[place, group * seq_dev + row] == me
                    count = count + named.astype(jnp.int32)
            counts[group] = count
            holder_counts[group] = 0
            return 0

        lax.fori_loop(0, group_count, scan_group, 0)

        def finish_group(group, found):
            for slot in range(slots):
                item = group * slots + slot
                here = slot < counts[group]
                entry = jnp.where(here, table[item], 0)
                row = entry // tail_pages
                sequence = group * seq_dev + row
                first = home_tokens + (entry - row * tail_pages) * page
                tokens = jnp.where(here, jnp.clip(lengths[sequence] - first, 0, page), 0)
                item_sequence[item] = sequence
                item_tokens[item] = tokens
                item_list[found] = item
                found = found + (tokens > 0).astype(jnp.int32)
            return found

        item_count[0] = lax.fori_loop(0, group_count, finish_group, jnp.int32(0))

        def own_row(row, _):
            length = lengths[me * seq_dev + row]
            for place in range(tail_pages):
                entry = row * tail_pages + place
                holder = routes[place, me * seq_dev + row]
                slot = holder_counts[holder]
                holder_counts[holder] = slot + 1
                entry_item[entry] = holder * slots + slot
                entry_ok[entry] = (home_tokens + place * page < length).astype(jnp.int32)
            return 0

        lax.fori_loop(0, seq_dev, own_row, 0)

        terms = absorbed_queries(queries[...], key_up[...], kv_heads)
        token, head_ok = row_masks(rows, kv_heads)
        for start in range(0, seq_dev, 4):
            part = range(start, min(start + 4, seq_dev))
            packed, lse = attend_all(
                [terms[row] for row in part],
                [resident[row] for row in part],
                [head_ok & (token < lengths[me * seq_dev + row]) for row in part],
            )
            for place, row in enumerate(part):
                packed_out[row] = packed[place]
                lse_out[row] = jnp.broadcast_to(lse[place], (pad_heads, lanes))

    def page_kernel(
        item_sequence, item_tokens, item_list, item_count, queries, key_up, overflow,
        out, pages, terms_ref, stats_ref, sems,
    ):
        items, rows, _ = overflow.shape
        slots = items // group_count
        kv_heads = key_up.shape[0] // half
        found = item_count[0]

        def copy_of(place):
            return pltpu.make_async_copy(
                overflow.at[item_list[place]], pages.at[place], sems.at[place]
            )

        def start_copy(place, _):
            copy_of(place).start()
            return 0

        lax.fori_loop(0, found, start_copy, 0)
        terms_ref[...] = absorbed_queries(queries[...], key_up[...], kv_heads)
        token, head_ok = row_masks(rows, kv_heads)
        stat_lane = lax.broadcasted_iota(jnp.int32, (pad_heads, lanes), 1)

        def one_batch(step, _):
            first = step * batch
            for offset in range(batch):
                @pl.when(first + offset < found)
                def _():
                    copy_of(first + offset).wait()

            places = [jnp.minimum(first + offset, found - 1) for offset in range(batch)]
            chosen = [item_list[place] for place in places]
            packed, lse = attend_all(
                [terms_ref[item_sequence[item]] for item in chosen],
                [pages[place] for place in places],
                [head_ok & (token < item_tokens[item]) for item in chosen],
            )
            for offset, item in enumerate(chosen):
                group = item // slots
                slot = item - group * slots
                out[group, slot] = packed[offset].astype(bf16)
                stats = stats_ref[group]
                for place, term in enumerate(three_terms(lse[offset])):
                    mine = stat_lane == slot * stat_lanes + place
                    stats = jnp.where(mine, term.astype(f32), stats)
                stats_ref[group] = stats
            return 0

        lax.fori_loop(0, (found + batch - 1) // batch, one_batch, 0)
        out[:, slots] = stats_ref[:, 0:8].astype(bf16)
        out[:, slots + 1] = stats_ref[:, 8:16].astype(bf16)

    def merge_kernel(entry_item, entry_ok, received, packed_home, lse_home, out, rows_ref):
        seq_dev = packed_home.shape[0]
        slots = received.shape[1] - 2
        tail_pages = entry_item.shape[0] // seq_dev
        lane8 = lax.broadcasted_iota(jnp.int32, (8, lanes), 1)
        lane16 = lax.broadcasted_iota(jnp.int32, (pad_heads, lanes), 1)
        is_term = (lane16 % stat_lanes) < 3
        slot_of_lane = lane16 // stat_lanes

        def spread(value):
            return jnp.where(lane8 < half, value[0:8], value[8:16])

        for row in range(seq_dev):
            parts = [(lse_home[row], packed_home[row])]
            for page_index in range(tail_pages):
                entry = row * tail_pages + page_index
                item = entry_item[entry]
                holder = item // slots
                slot = item - holder * slots
                stats = jnp.concatenate(
                    [received[holder, slots].astype(f32), received[holder, slots + 1].astype(f32)],
                    axis=0,
                )
                mine = is_term & (slot_of_lane == slot)
                lse = jnp.sum(jnp.where(mine, stats, 0.0), axis=1, keepdims=True)
                lse = jnp.where(entry_ok[entry] > 0, lse, very_low)
                lse = jnp.broadcast_to(lse, (pad_heads, lanes))
                packed = jnp.where(entry_ok[entry] > 0, received[holder, slot].astype(f32), 0.0)
                parts.append((lse, packed))
            peak = parts[0][0]
            for lse, _ in parts[1:]:
                peak = jnp.maximum(peak, lse)
            total = jnp.zeros((8, lanes), f32)
            merged = jnp.zeros((8, lanes), f32)
            for lse, packed in parts:
                factor = spread(jnp.exp2(lse - peak))
                total = total + factor
                merged = merged + factor * packed
            rows_ref[row * 8 : (row + 1) * 8, :] = merged / total
        for query in range(8):
            block = rows_ref[pl.ds(query, seq_dev, stride=8), :].astype(bf16)
            for target in range(group_count):
                out[target, query] = block

    def project_kernel(received, value_up, weight, out):
        sequences = received.shape[0] * received.shape[2]
        kv_heads = value_up.shape[1] // lanes
        pieces = [
            jnp.dot(
                received[:, query].astype(f32).reshape(sequences, lanes).astype(bf16),
                value_up[...],
                preferred_element_type=f32,
            )
            for query in range(8)
        ]
        attended = jnp.concatenate(
            [
                piece[:, head * lanes : (head + 1) * lanes]
                for head in range(kv_heads)
                for piece in pieces
            ],
            axis=1,
        )
        high = attended.astype(bf16)
        low = (attended - high.astype(f32)).astype(bf16)
        both = jnp.concatenate([high, low], axis=0)
        result = jnp.dot(both, weight[...], preferred_element_type=f32)
        out[...] = (result[:sequences] + result[sequences:]).astype(bf16)

    def body(
        queries, resident_cache, overflow_cache, key_up_weight, value_up_weight,
        lengths, routes, out_weight,
    ):
        seq_dev, head_dev, head_size = queries.shape
        kv_heads, width, _ = key_up_weight.shape
        slots = overflow_cache.shape[2]
        page = overflow_cache.shape[3]
        items = group_count * slots
        tail_pages = routes.shape[1]
        home_tokens = resident_cache.shape[1]
        smem = pl.BlockSpec(memory_space=pltpu.SMEM)
        vmem = pl.BlockSpec(memory_space=pltpu.VMEM)
        hbm = pl.BlockSpec(memory_space=pl.ANY)
        ints = lambda size: jax.ShapeDtypeStruct((size,), jnp.int32)
        own = lax.axis_index("dp").astype(jnp.int32).reshape(1)
        flat_routes = routes[:, :, 0].T
        key_up = key_up_weight.reshape(kv_heads * width, head_size)
        flat_queries = queries.reshape(seq_dev * head_dev, head_size)

        spread_queries = jnp.broadcast_to(
            flat_queries[None], (group_count,) + flat_queries.shape
        )
        all_queries = lax.all_to_all(
            spread_queries, "dp", split_axis=0, concat_axis=0, tiled=True
        ).reshape(-1, head_size)

        entries = seq_dev * tail_pages
        (
            item_sequence, item_tokens, item_list, item_count, entry_item, entry_ok,
            packed_home, lse_home,
        ) = pl.pallas_call(
            home_kernel,
            out_shape=(
                ints(items), ints(items), ints(items), ints(1), ints(entries), ints(entries),
                near((seq_dev, 8, lanes), f32),
                near((seq_dev, pad_heads, lanes), f32),
            ),
            in_specs=[smem, smem, smem, vmem, vmem, vmem],
            out_specs=(smem, smem, smem, smem, smem, smem, vmem, vmem),
            scratch_shapes=[
                pltpu.SMEM((items + 8,), jnp.int32),
                pltpu.SMEM((group_count,), jnp.int32),
                pltpu.SMEM((group_count,), jnp.int32),
            ],
            cost_estimate=pl.CostEstimate(
                flops=200_000_000, transcendentals=0, bytes_accessed=1 << 20
            ),
        )(
            flat_routes, lengths, own, flat_queries, key_up,
            resident_cache.reshape(seq_dev, home_tokens * kv_heads, lanes),
        )

        partials = pl.pallas_call(
            page_kernel,
            out_shape=near((group_count, slots + 2, 8, lanes), bf16),
            in_specs=[smem, smem, smem, smem, vmem, vmem, hbm],
            out_specs=vmem,
            scratch_shapes=[
                pltpu.VMEM((items, page * kv_heads, lanes), bf16),
                pltpu.VMEM((group_count * seq_dev, 48, lanes), bf16),
                pltpu.VMEM((group_count, pad_heads, lanes), f32),
                pltpu.SemaphoreType.DMA((items,)),
            ],
        )(
            item_sequence, item_tokens, item_list, item_count, pin(all_queries), key_up,
            overflow_cache.reshape(items, page * kv_heads, lanes),
        )
        partials = lax.all_to_all(partials, "dp", split_axis=0, concat_axis=0, tiled=True)

        merged = pl.pallas_call(
            merge_kernel,
            out_shape=near((group_count, 8, seq_dev, lanes), bf16),
            in_specs=[smem, smem, vmem, vmem, vmem],
            out_specs=vmem,
            scratch_shapes=[pltpu.VMEM((seq_dev * 8, lanes), f32)],
        )(entry_item, entry_ok, pin(partials), pin(packed_home), pin(lse_home))
        merged = lax.all_to_all(merged, "dp", split_axis=0, concat_axis=0, tiled=True)

        blocks = jnp.eye(kv_heads, dtype=bf16)[:, None, :, None] * value_up_weight[:, :, None, :]
        blocks = blocks.reshape(kv_heads * width, kv_heads * head_size)
        blocks = jnp.pad(blocks, ((0, lanes - kv_heads * width), (0, 0)))
        sequences = group_count * seq_dev
        partial_out = pl.pallas_call(
            project_kernel,
            out_shape=near((sequences, out_weight.shape[1]), bf16),
            in_specs=[vmem, vmem, vmem],
            out_specs=vmem,
        )(pin(merged), blocks, out_weight)
        pieces = lax.all_to_all(
            partial_out.reshape(head_parts, sequences // head_parts, -1),
            "mp", split_axis=0, concat_axis=0, tiled=True,
        )
        return jnp.sum(pieces.astype(f32), axis=0).astype(bf16)

    placed = (
        P("dp", "mp", None),
        P("dp", None, "mp", None),
        P("dp", None, None, None, "mp", None),
        P("mp", None, None),
        P("mp", None, None),
        P(),
        P(),
        P("mp", "dp"),
    )
    return jax.shard_map(body, mesh=mesh, in_specs=placed, out_specs=P("mp", "dp"), check_vma=False)
```

time: 78.4 us -> 58.1 us (0.74)
  Pallas kernels: 33.2 us -> 14.6 us
  blocking collectives: 20.6 us -> 18.5 us
  waiting for transfers between devices: 7.5 us -> 9.23 us
  local copies, waits for them, and re-layouts: 4.95 us -> 3.4 us
    pallas_call x4, Pallas kernels: 33.2 us -> 14.6 us  [the longest x1 4.91 us: body(): pl.pallas_call(home_kernel, out_shape=(ints(items), ints(items), ints(ite...]
    all_to_all x1, waiting for transfers between devices: 1 us -> 2.73 us  [body(): lax.all_to_all(spread_queries, 'dp', split_axis=0, concat_axis=0, tiled=T...]
    all_to_all x1, blocking collectives: 12.7 us -> 11.4 us  [body(): lax.all_to_all(partials, 'dp', split_axis=0, concat_axis=0, tiled=True)]
    unnamed x8 -> x4, local copies, waits for them, and re-layouts: 2.75 us -> 1.91 us
  transfers between devices with their start and end apart: 2 -> 2, of which waited for: 2 -> 2; matrix products, arithmetic and copies ran while one was open for 3% -> 4% of each run, Pallas kernels for 8% -> 9%
where the time goes in v2:
time: 58.1 us; the launch traced here: 57.3 us
  blocking collectives  18.5 us (32%)
  Pallas kernels  14.6 us (25%)
  starting transfers between devices  10.7 us (18%)
  waiting for transfers between devices  9.23 us (16%)
  local copies, waits for them, and re-layouts  3.4 us (6%)
  other arithmetic  0.76 us (1%)
    all_to_all x1, blocking collectives, body(): lax.all_to_all(partials, 'dp', split_axis=0, concat_axis=0, tiled=True)  11.4 us
    all_to_all x1, starting transfers between devices, body(): lax.all_to_all(spread_queries, 'dp', split_axis=0, concat_axis=0, tiled=T...  7.31 us
    all_to_all x1, blocking collectives, body(): lax.all_to_all(partial_out.reshape(head_parts, sequences // head_parts, -...  7.15 us
    all_to_all x1, waiting for transfers between devices, body(): lax.all_to_all(merged, 'dp', split_axis=0, concat_axis=0, tiled=True)  6.5 us
    pallas_call x1, Pallas kernels, body(): pl.pallas_call(home_kernel, out_shape=(ints(items), ints(items), ints(ite...  4.91 us
    pallas_call x1, Pallas kernels, body(): pl.pallas_call(page_kernel, out_shape=near((group_count, slots + 2, 8, la...  4.86 us
    all_to_all x1, starting transfers between devices, body(): lax.all_to_all(merged, 'dp', split_axis=0, concat_axis=0, tiled=True)  3.37 us
    pallas_call x1, Pallas kernels, body(): pl.pallas_call(project_kernel, out_shape=near((sequences, out_weight.shap...  3.05 us
  transfers between devices with their start and end apart: 2, of which 2 were waited for; matrix products, arithmetic and copies ran while one was open for 4% of the time, Pallas kernels for 9%

profile of v2, /device:TPU:0, one launch (start us, length us, event | category | flops | bytes accessed | tf_op | source)
XLA Modules:
  0.0 57.3 jit_solution(10126450265167996724)
XLA Ops:
  0.0 0.0 copy-start
  0.0 1.5 %broadcast_in_dim.2 = bf16[8,128,128]{2,1,0:T(8,128)(2,1)} broadcast(bf16[128,128]{1,0:T(8,128)(2,1)} %bitcast.25), dimensions={1,2} | broadcast | bytes 294912 | tf_op jit(solution)/shard_map/broadcast_in_dim | solution.py:309
  1.5 7.3 %all-to-all-start = ((bf16[8,128,128]{2,1,0:T(8,128)(2,1)}), bf16[8,128,128]{2,1,0:T(8,128)(2,1)S(1)}, u32[]{:S(2)}, u32[]{:S(2)}) async-start(bf16[8,128,128]{2,1,0:T(8,128)(2,1)} %broadcast_in_dim.2), calls=%async_computation | async-start | bytes 524288 | tf_op jit(solution)/shard_map/all_to_all | solution.py:312
  8.8 1.3 %copy.14 = s32[64,6,1]{0,1,2:T(8,128)} copy(s32[64,6,1]{0,2,1:T(1,128)} %param.14) | data formatting | bytes 3072
  10.1 4.9 %shard_map.82 = (s32[64]{0:T(128)}, s32[64]{0:T(128)}, s32[64]{0:T(128)}, s32[1]{0:T(128)}, s32[48]{0:T(128)}, /*index=5*/s32[48]{0:T(128)}, f32[8,8,128]{2,1,0:T(8,128)S(1)}, f32[8,16,128]{2,1,0:T(8,128)S(1)}) custom-call(s32[6,64]{1,0:T(8,128)} %bitcast.27, s32[64]{0:T(128)} %lengths.1, s32[1]{0:T(128)} %bitcast.1.own, bf16[128,128]{1,0:T(8,128)(2,1)} %bitcast.26, ...), custom_call_target="tpu_custom_call" | custom-call | flops 200000000 | bytes 1048576 | tf_op jit(solution)/shard_map/pallas_call | solution.py:320
  15.0 2.7 %all-to-all-done = bf16[8,128,128]{2,1,0:T(8,128)(2,1)S(1)} async-done(((bf16[8,128,128]{2,1,0:T(8,128)(2,1)}), bf16[8,128,128]{2,1,0:T(8,128)(2,1)S(1)}, u32[]{:S(2)}, u32[]{:S(2)}) %all-to-all-start) | async-done | bytes 262176 | tf_op jit(solution)/shard_map/all_to_all | solution.py:312
  17.7 4.9 %shard_map.83 = bf16[8,10,8,128]{3,2,1,0:T(8,128)(2,1)S(1)} custom-call(s32[64]{0:T(128)} %get-tuple-element.15.item_sequence, s32[64]{0:T(128)} %get-tuple-element.16.item_tokens, s32[64]{0:T(128)} %get-tuple-element.17.item_list, s32[1]{0:T(128)} %get-tuple-element.18.item_count, bf16[1024,128]{1,0:T(8,128)(2,1)S(1)} %bitcast.17, ...), custom_call_target="tpu_custom_call" | custom-call | tf_op jit(solution)/shard_map/pallas_call | solution.py:342
  22.6 11.4 %all_to_all.20.received = bf16[8,10,8,128]{3,2,1,0:T(8,128)(2,1)S(1)} all-to-all(bf16[8,10,8,128]{3,2,1,0:T(8,128)(2,1)S(1)} %shard_map.83), channel_id=1, replica_groups=mesh['dp'=8,'mp'=4] {'dp'}, dimensions={0} | all-to-all | bytes 327680 | tf_op jit(solution)/shard_map/all_to_all | solution.py:357
  34.0 1.8 %shard_map.84 = bf16[8,8,8,128]{3,2,1,0:T(8,128)(2,1)} custom-call(s32[48]{0:T(128)} %get-tuple-element.13.entry_item, s32[48]{0:T(128)} %get-tuple-element.14.entry_ok, bf16[8,10,8,128]{3,2,1,0:T(8,128)(2,1)S(1)} %all_to_all.20.received, f32[8,8,128]{2,1,0:T(8,128)S(1)} %get-tuple-element.19.packed_home, f32[8,16,128]{2,1,0:T(8,128)S(1)} %get-tuple-element.20.lse_home), custom_call_target="tpu_custom_call" | custom-call | tf_op jit(solution)/shard_map/pallas_call | solution.py:359
  35.8 3.4 %all-to-all-start.2 = ((bf16[8,8,8,128]{3,2,1,0:T(8,128)(2,1)}), bf16[8,8,8,128]{3,2,1,0:T(8,128)(2,1)S(1)}, u32[]{:S(2)}, u32[]{:S(2)}) async-start(bf16[8,8,8,128]{3,2,1,0:T(8,128)(2,1)} %shard_map.84), calls=%async_computation.2 | async-start | bytes 262144 | tf_op jit(solution)/shard_map/all_to_all | solution.py:366
  39.2 0.0 copy-done
  39.2 0.1 broadcast_multiply_fusion
  39.3 0.6 %copy.13 = bf16[16,8,2,128]{3,1,2,0:T(8,128)(2,1)} copy(bf16[16,8,2,128]{3,2,1,0:T(2,128)(2,1)S(1)} %bitcast.22) | data formatting | bytes 131072
  39.9 6.5 %all-to-all-done.2.received = bf16[8,8,8,128]{3,2,1,0:T(8,128)(2,1)S(1)} async-done(((bf16[8,8,8,128]{3,2,1,0:T(8,128)(2,1)}), bf16[8,8,8,128]{3,2,1,0:T(8,128)(2,1)S(1)}, u32[]{:S(2)}, u32[]{:S(2)}) %all-to-all-start.2) | async-done | bytes 131104 | tf_op jit(solution)/shard_map/all_to_all | solution.py:366
  46.4 3.0 %shard_map.85 = bf16[64,1024]{1,0:T(8,128)(2,1)S(1)} custom-call(bf16[8,8,8,128]{3,2,1,0:T(8,128)(2,1)S(1)} %all-to-all-done.2.received, bf16[128,256]{1,0:T(8,128)(2,1)} %bitcast.21, bf16[2048,1024]{1,0:T(8,128)(2,1)} %weight.1), custom_call_target="tpu_custom_call" | custom-call | tf_op jit(solution)/shard_map/pallas_call | solution.py:372
  49.5 7.2 %all_to_all.21 = bf16[4,16,1024]{2,1,0:T(8,128)(2,1)S(1)} all-to-all(bf16[4,16,1024]{2,1,0:T(8,128)(2,1)S(1)} %bitcast.18), channel_id=1, replica_groups=mesh['dp'=8,'mp'=4] {'mp'}, dimensions={0} | all-to-all | bytes 262144 | tf_op jit(solution)/shard_map/all_to_all | solution.py:378
  56.7 0.6 %reduce_sum.12 = bf16[16,1024]{1,0:T(8,128)(2,1)} reduce(bf16[4,16,1024]{2,1,0:T(8,128)(2,1)S(1)} %all_to_all.21, bf16[]{:T(256)} %constant.9.clone.1), dimensions={0}, to_apply=%region_0.1 | reduce | flops 49152 | bytes 163842 | tf_op jit(solution)/shard_map/reduce_sum | solution.py:382
  (1 shorter events, 0.0 us)
Async XLA Ops:
  0.0 39.2 %copy-start = (bf16[2,64,128]{2,1,0:T(8,128)(2,1)S(1)}, bf16[2,64,128]{2,1,0:T(8,128)(2,1)}, u32[]{:S(2)}) copy-start(bf16[2,64,128]{2,1,0:T(8,128)(2,1)} %param.12) | copy-start | bytes 98308
  1.5 16.2 %all-to-all-start = ((bf16[8,128,128]{2,1,0:T(8,128)(2,1)}), bf16[8,128,128]{2,1,0:T(8,128)(2,1)S(1)}, u32[]{:S(2)}, u32[]{:S(2)}) async-start(bf16[8,128,128]{2,1,0:T(8,128)(2,1)} %broadcast_in_dim.2), calls=%async_computation | async-start | bytes 524288 | tf_op jit(solution)/shard_map/all_to_all | solution.py:312
  35.8 10.7 %all-to-all-start.2 = ((bf16[8,8,8,128]{3,2,1,0:T(8,128)(2,1)}), bf16[8,8,8,128]{3,2,1,0:T(8,128)(2,1)S(1)}, u32[]{:S(2)}, u32[]{:S(2)}) async-start(bf16[8,8,8,128]{3,2,1,0:T(8,128)(2,1)} %shard_map.84), calls=%async_computation.2 | async-start | bytes 262144 | tf_op jit(solution)/shard_map/all_to_all | solution.py:366

commit v3 on v2

--- a/solution.py
+++ b/solution.py
@@ -87,6 +87,10 @@
     return pltpu.with_memory_space_constraint(array, pltpu.VMEM)
 
 
+def far(array):
+    return pltpu.with_memory_space_constraint(array, pltpu.HBM)
+
+
 def near(shape, kind):
     return pltpu.VMEM(shape, kind)
 
@@ -96,11 +100,14 @@
     head_parts = mesh.shape["mp"]
 
     def home_kernel(
-        routes, lengths, own, queries, key_up, resident,
+        routes, lengths, own, queries, key_up, value_up, resident_far,
         item_sequence, item_tokens, item_list, item_count, entry_item, entry_ok,
-        packed_out, lse_out, table, counts, holder_counts,
+        packed_out, lse_out, blocks, key_near,
+        table, counts, holder_counts, resident, home_sem,
     ):
         seq_dev, rows, _ = resident.shape
+        home_copy = pltpu.make_async_copy(resident_far, resident, home_sem)
+        home_copy.start()
         kv_heads = key_up.shape[0] // half
         items = item_sequence.shape[0]
         slots = items // group_count
@@ -114,7 +121,7 @@
             for row in range(seq_dev):
                 for place in range(tail_pages):
                     table[group * slots + count] = row * tail_pages + place
-                    named = routes[place, group * seq_dev + row] == me
+                    named = routes[place, 0, group * seq_dev + row] == me
                     count = count + named.astype(jnp.int32)
             counts[group] = count
             holder_counts[group] = 0
@@ -143,7 +150,7 @@
             length = lengths[me * seq_dev + row]
             for place in range(tail_pages):
                 entry = row * tail_pages + place
-                holder = routes[place, me * seq_dev + row]
+                holder = routes[place, 0, me * seq_dev + row]
                 slot = holder_counts[holder]
                 holder_counts[holder] = slot + 1
                 entry_item[entry] = holder * slots + slot
@@ -152,8 +159,14 @@
 
         lax.fori_loop(0, seq_dev, own_row, 0)
 
+        key_near[...] = key_up[...]
+        blocks[...] = jnp.zeros(blocks.shape, bf16)
+        for head in range(kv_heads):
+            across = slice(head * lanes, (head + 1) * lanes)
+            blocks[head * half : (head + 1) * half, across] = value_up[head]
         terms = absorbed_queries(queries[...], key_up[...], kv_heads)
         token, head_ok = row_masks(rows, kv_heads)
+        home_copy.wait()
         for start in range(0, seq_dev, 4):
             part = range(start, min(start + 4, seq_dev))
             packed, lse = attend_all(
@@ -261,7 +274,8 @@
             for target in range(group_count):
                 out[target, query] = block
 
-    def project_kernel(received, value_up, weight, out):
+    def project_kernel(own, received, value_up, weight, *rest):
+        outs, out = rest[:head_parts], rest[head_parts]
         sequences = received.shape[0] * received.shape[2]
         kv_heads = value_up.shape[1] // lanes
         pieces = [
@@ -284,7 +298,9 @@
         low = (attended - high.astype(f32)).astype(bf16)
         both = jnp.concatenate([high, low], axis=0)
         result = jnp.dot(both, weight[...], preferred_element_type=f32)
-        out[...] = (result[:sequences] + result[sequences:]).astype(bf16)
+        out[...] = (result[:sequences] + result[sequences:]).astype(bf16).reshape(out.shape)
+        for step in range(head_parts):
+            outs[step][...] = out[(own[1] + step) % head_parts]
 
     def body(
         queries, resident_cache, overflow_cache, key_up_weight, value_up_weight,
@@ -299,10 +315,11 @@
         home_tokens = resident_cache.shape[1]
         smem = pl.BlockSpec(memory_space=pltpu.SMEM)
         vmem = pl.BlockSpec(memory_space=pltpu.VMEM)
-        hbm = pl.BlockSpec(memory_space=pl.ANY)
+        hbm = pl.BlockSpec(memory_space=pltpu.HBM)
+        small = pltpu.CompilerParams(vmem_limit_bytes=16 << 20)
         ints = lambda size: jax.ShapeDtypeStruct((size,), jnp.int32)
-        own = lax.axis_index("dp").astype(jnp.int32).reshape(1)
-        flat_routes = routes[:, :, 0].T
+        own = jnp.stack([lax.axis_index("dp"), lax.axis_index("mp")]).astype(jnp.int32)
+        flat_routes = routes.transpose(1, 2, 0)
         key_up = key_up_weight.reshape(kv_heads * width, head_size)
         flat_queries = queries.reshape(seq_dev * head_dev, head_size)
 
@@ -316,26 +333,30 @@
         entries = seq_dev * tail_pages
         (
             item_sequence, item_tokens, item_list, item_count, entry_item, entry_ok,
-            packed_home, lse_home,
+            packed_home, lse_home, blocks, key_near,
         ) = pl.pallas_call(
             home_kernel,
             out_shape=(
                 ints(items), ints(items), ints(items), ints(1), ints(entries), ints(entries),
                 near((seq_dev, 8, lanes), f32),
                 near((seq_dev, pad_heads, lanes), f32),
+                near((lanes, kv_heads * head_size), bf16),
+                near(key_up.shape, bf16),
             ),
-            in_specs=[smem, smem, smem, vmem, vmem, vmem],
-            out_specs=(smem, smem, smem, smem, smem, smem, vmem, vmem),
+            in_specs=[smem, smem, smem, vmem, vmem, vmem, hbm],
+            out_specs=(smem,) * 6 + (vmem,) * 4,
             scratch_shapes=[
                 pltpu.SMEM((items + 8,), jnp.int32),
                 pltpu.SMEM((group_count,), jnp.int32),
                 pltpu.SMEM((group_count,), jnp.int32),
+                pltpu.VMEM((seq_dev, home_tokens * kv_heads, lanes), bf16),
+                pltpu.SemaphoreType.DMA,
             ],
             cost_estimate=pl.CostEstimate(
                 flops=200_000_000, transcendentals=0, bytes_accessed=1 << 20
             ),
         )(
-            flat_routes, lengths, own, flat_queries, key_up,
+            flat_routes, lengths, own, flat_queries, key_up, value_up_weight,
             resident_cache.reshape(seq_dev, home_tokens * kv_heads, lanes),
         )
 
@@ -350,9 +371,10 @@
                 pltpu.VMEM((group_count, pad_heads, lanes), f32),
                 pltpu.SemaphoreType.DMA((items,)),
             ],
+            compiler_params=small,
         )(
-            item_sequence, item_tokens, item_list, item_count, pin(all_queries), key_up,
-            overflow_cache.reshape(items, page * kv_heads, lanes),
+            item_sequence, item_tokens, item_list, item_count, pin(all_queries), pin(key_near),
+            far(overflow_cache.reshape(items, page * kv_heads, lanes)),
         )
         partials = lax.all_to_all(partials, "dp", split_axis=0, concat_axis=0, tiled=True)
 
@@ -362,24 +384,28 @@
             in_specs=[smem, smem, vmem, vmem, vmem],
             out_specs=vmem,
             scratch_shapes=[pltpu.VMEM((seq_dev * 8, lanes), f32)],
+            compiler_params=small,
         )(entry_item, entry_ok, pin(partials), pin(packed_home), pin(lse_home))
         merged = lax.all_to_all(merged, "dp", split_axis=0, concat_axis=0, tiled=True)
 
-        blocks = jnp.eye(kv_heads, dtype=bf16)[:, None, :, None] * value_up_weight[:, :, None, :]
-        blocks = blocks.reshape(kv_heads * width, kv_heads * head_size)
-        blocks = jnp.pad(blocks, ((0, lanes - kv_heads * width), (0, 0)))
         sequences = group_count * seq_dev
-        partial_out = pl.pallas_call(
+        width_out = out_weight.shape[1]
+        piece = (sequences // head_parts, width_out)
+        pieces = pl.pallas_call(
             project_kernel,
-            out_shape=near((sequences, out_weight.shape[1]), bf16),
-            in_specs=[vmem, vmem, vmem],
-            out_specs=vmem,
-        )(pin(merged), blocks, out_weight)
-        pieces = lax.all_to_all(
-            partial_out.reshape(head_parts, sequences // head_parts, -1),
-            "mp", split_axis=0, concat_axis=0, tiled=True,
-        )
-        return jnp.sum(pieces.astype(f32), axis=0).astype(bf16)
+            out_shape=(near(piece, bf16),) * head_parts,
+            in_specs=[smem, vmem, vmem, vmem],
+            out_specs=(vmem,) * head_parts,
+            scratch_shapes=[
+                pltpu.VMEM((head_parts,) + piece, bf16),
+            ],
+            compiler_params=small,
+        )(own, pin(merged), pin(blocks), out_weight)
+        total = pieces[0].astype(f32)
+        for step in range(1, head_parts):
+            ring = [(source, (source + step) % head_parts) for source in range(head_parts)]
+            total = total + lax.ppermute(pieces[step], "mp", ring).astype(f32)
+        return total.astype(bf16)
 
     placed = (
         P("dp", "mp", None),

time: 58.1 us -> 54.2 us (0.933)
  waiting for transfers between devices: 9.23 us -> 5.06 us
  blocking collectives: 18.5 us -> 20.1 us
  Pallas kernels: 14.6 us -> 13.1 us
    all_to_all x1 -> x0, waiting for transfers between devices: 6.5 us -> none  [body(): lax.all_to_all(merged, 'dp', split_axis=0, concat_axis=0, tiled=True)]
    all_to_all x1 -> x0, starting transfers between devices: 3.37 us -> none  [body(): lax.all_to_all(merged, 'dp', split_axis=0, concat_axis=0, tiled=True)]
    ppermute x0 -> x3, starting transfers between devices: none -> 2.98 us  [body(): total = total + lax.ppermute(pieces[step], 'mp', ring).astype(f32)]
    all_to_all x1, blocking collectives: 7.15 us -> 9.74 us  [body(): lax.all_to_all(merged, 'dp', split_axis=0, concat_axis=0, tiled=True)]
    pallas_call x1, Pallas kernels: 3.05 us -> 1.4 us  [body(): pl.pallas_call(project_kernel, out_shape=(near(piece, bf16),) * head_part...]
    ppermute x0 -> x3, waiting for transfers between devices: none -> 1.6 us  [body(): total = total + lax.ppermute(pieces[step], 'mp', ring).astype(f32)]
    all_to_all x1, blocking collectives: 11.4 us -> 10.3 us  [body(): lax.all_to_all(partials, 'dp', split_axis=0, concat_axis=0, tiled=True)]
    pallas_call x1, Pallas kernels: 4.86 us -> 5.81 us  [body(): pl.pallas_call(page_kernel, out_shape=near((group_count, slots + 2, 8, la...]
  transfers between devices with their start and end apart: 2 -> 4, of which waited for: 2 -> 4; matrix products, arithmetic and copies ran while one was open for 4% -> 1% of each run, Pallas kernels for 9% -> 9%
where the time goes in v3:
time: 54.2 us; the launch traced here: 53.6 us
  blocking collectives  20.1 us (37%)
  Pallas kernels  13.1 us (24%)
  starting transfers between devices  10.3 us (19%)
  waiting for transfers between devices  5.06 us (9%)
  local copies, waits for them, and re-layouts  3.79 us (7%)
  other arithmetic  1.24 us (2%)
    all_to_all x1, blocking collectives, body(): lax.all_to_all(partials, 'dp', split_axis=0, concat_axis=0, tiled=True)  10.3 us
    all_to_all x1, blocking collectives, body(): lax.all_to_all(merged, 'dp', split_axis=0, concat_axis=0, tiled=True)  9.74 us
    all_to_all x1, starting transfers between devices, body(): lax.all_to_all(spread_queries, 'dp', split_axis=0, concat_axis=0, tiled=T...  7.31 us
    pallas_call x1, Pallas kernels, body(): pl.pallas_call(page_kernel, out_shape=near((group_count, slots + 2, 8, la...  5.81 us
    pallas_call x1, Pallas kernels, body(): pl.pallas_call(home_kernel, out_shape=(ints(items), ints(items), ints(ite...  4.82 us
    all_to_all x1, waiting for transfers between devices, body(): lax.all_to_all(spread_queries, 'dp', split_axis=0, concat_axis=0, tiled=T...  3.46 us
    ppermute x3, starting transfers between devices, body(): total = total + lax.ppermute(pieces[step], 'mp', ring).astype(f32)  2.98 us
    unnamed x14, local copies, waits for them, and re-layouts  2.31 us
  transfers between devices with their start and end apart: 4, of which 4 were waited for; matrix products, arithmetic and copies ran while one was open for 1% of the time, Pallas kernels for 9%

profile of v3, /device:TPU:0, one launch (start us, length us, event | category | flops | bytes accessed | tf_op | source)
XLA Modules:
  0.0 53.6 jit_solution(9883930645695869145)
XLA Ops:
  0.0 1.5 %broadcast_in_dim.2 = bf16[8,128,128]{2,1,0:T(8,128)(2,1)} broadcast(bf16[128,128]{1,0:T(8,128)(2,1)} %bitcast.11), dimensions={1,2} | broadcast | bytes 294912 | tf_op jit(solution)/shard_map/broadcast_in_dim | solution.py:326
  1.5 7.3 %all-to-all-start = ((bf16[8,128,128]{2,1,0:T(8,128)(2,1)}), bf16[8,128,128]{2,1,0:T(8,128)(2,1)S(1)}, u32[]{:S(2)}, u32[]{:S(2)}) async-start(bf16[8,128,128]{2,1,0:T(8,128)(2,1)} %broadcast_in_dim.2), calls=%async_computation | async-start | bytes 524288 | tf_op jit(solution)/shard_map/all_to_all | solution.py:329
  8.8 0.6 %pad_add_fusion.own = s32[2]{0:T(128)} fusion(s32[1]{0:T(128)} %bitcast.1, s32[1]{0:T(128)} %bitcast), kind=kLoop, calls=%fused_computation.1 | loop fusion | flops 2 | bytes 16 | tf_op jit(solution)/shard_map/stack | solution.py:321
  9.4 4.8 %shard_map.82 = (s32[64]{0:T(128)}, s32[64]{0:T(128)}, s32[64]{0:T(128)}, s32[1]{0:T(128)}, s32[48]{0:T(128)}, /*index=5*/s32[48]{0:T(128)}, f32[8,8,128]{2,1,0:...) custom-call(s32[6,1,64]{2,1,0:T(1,128)} %bitcast.14, s32[64]{0:T(128)} %lengths.1, ...), custom_call_target="tpu_custom_call" | custom-call | flops 200000000 | bytes 1048576 | tf_op jit(solution)/shard_map/pallas_call | solution.py:337
  14.2 0.0 copy-start.2
  14.2 0.0 copy-start.3
  14.3 3.5 %all-to-all-done = bf16[8,128,128]{2,1,0:T(8,128)(2,1)S(1)} async-done(((bf16[8,128,128]{2,1,0:T(8,128)(2,1)}), bf16[8,128,128]{2,1,0:T(8,128)(2,1)S(1)}, u32[]{:S(2)}, u32[]{:S(2)}) %all-to-all-start) | async-done | bytes 262176 | tf_op jit(solution)/shard_map/all_to_all | solution.py:329
  17.7 0.8 %copy-done.4 = s32[64]{0:T(128)S(1)} copy-done((s32[64]{0:T(128)S(1)}, s32[64]{0:T(128)}, u32[]{:S(2)}) %copy-start.4) | copy-done | bytes 280
  18.5 0.8 %copy-done.5 = s32[64]{0:T(128)S(1)} copy-done((s32[64]{0:T(128)S(1)}, s32[64]{0:T(128)}, u32[]{:S(2)}) %copy-start.5) | copy-done | bytes 280
  19.3 0.7 %copy-done.6 = s32[64]{0:T(128)S(1)} copy-done((s32[64]{0:T(128)S(1)}, s32[64]{0:T(128)}, u32[]{:S(2)}) %copy-start.6) | copy-done | bytes 280
  20.0 5.8 %shard_map.83 = bf16[8,10,8,128]{3,2,1,0:T(8,128)(2,1)S(1)} custom-call(s32[64]{0:T(128)S(1)} %copy-done.4, s32[64]{0:T(128)S(1)} %copy-done.5, s32[64]{0:T(128)S(1)} %copy-done.6, s32[1]{0:T(128)} %get-tuple-element.24.item_count, bf16[1024,128]{1,0:T(8,128)(2,1)S(1)} %bitcast.8, bf16[128,128]{1,0:T(8,128)(2,1)S(1)} %get-tuple-element.25.key_up, ...), custom_call_target="tpu_custom_call" | custom-call | tf_op jit(solution)/shard_map/pallas_call | solution.py:363
  25.8 10.3 %all_to_all.15.received = bf16[8,10,8,128]{3,2,1,0:T(8,128)(2,1)S(1)} all-to-all(bf16[8,10,8,128]{3,2,1,0:T(8,128)(2,1)S(1)} %shard_map.83), channel_id=1, replica_groups=mesh['dp'=8,'mp'=4] {'dp'}, dimensions={0} | all-to-all | bytes 327680 | tf_op jit(solution)/shard_map/all_to_all | solution.py:379
  36.1 0.0 copy-done.2
  36.2 0.0 copy-done.3
  36.2 1.0 %shard_map.84 = bf16[8,8,8,128]{3,2,1,0:T(8,128)(2,1)S(1)} custom-call(s32[48]{0:T(128)S(1)} %copy-done.2, s32[48]{0:T(128)S(1)} %copy-done.3, bf16[8,10,8,128]{3,2,1,0:T(8,128)(2,1)S(1)} %all_to_all.15.received, f32[8,8,128]{2,1,0:T(8,128)S(1)} %get-tuple-element.26.packed_home, f32[8,16,128]{2,1,0:T(8,128)S(1)} %get-tuple-element.27.lse_home), custom_call_target="tpu_custom_call" | custom-call | tf_op jit(solution)/shard_map/pallas_call | solution.py:381
  37.2 9.7 %all_to_all.16.received = bf16[8,8,8,128]{3,2,1,0:T(8,128)(2,1)S(1)} all-to-all(bf16[8,8,8,128]{3,2,1,0:T(8,128)(2,1)S(1)} %shard_map.84), channel_id=1, replica_groups=mesh['dp'=8,'mp'=4] {'dp'}, dimensions={0} | all-to-all | bytes 262144 | tf_op jit(solution)/shard_map/all_to_all | solution.py:389
  46.9 1.4 %shard_map.85 = (bf16[16,1024]{1,0:T(8,128)(2,1)S(1)}, bf16[16,1024]{1,0:T(8,128)(2,1)S(1)}, bf16[16,1024]{1,0:T(8,128)(2,1)S(1)}, bf16[16,1024]{1,0:T(8,128)(2,1)S(1)}) custom-call(s32[2]{0:T(128)S(1)} %copy-done.1, bf16[8,8,8,128]{3,2,1,0:T(8,128)(2,1)S(1)} %all_to_all.16.received, bf16[128,256]{1,0:T(8,128)(2,1)S(1)} %get-tuple-element.28.value_up, ...), custom_call_target="tpu_custom_call" | custom-call | tf_op jit(solution)/shard_map/pallas_call | solution.py:394
  48.3 0.1 collective-permute-start
  48.4 1.5 %collective-permute-start.1 = (bf16[16,1024]{1,0:T(8,128)(2,1)S(1)}, bf16[16,1024]{1,0:T(8,128)(2,1)S(1)}, u32[]{:S(2)}, u32[]{:S(2)}) collective-permute-start(bf16[16,1024]{1,0:T(8,128)(2,1)S(1)} %get-tuple-element.31), channel_id=1, source_target_pairs={{0,2},{1,3},{2,0},{3,1},{4,6},{5,7},{6,4},{7,5},{8,10},{9,11},{10,... | collective-permute-start | bytes 98312 | tf_op jit(solution)/shard_map/ppermute | solution.py:407
  49.9 1.4 %collective-permute-start.2 = (bf16[16,1024]{1,0:T(8,128)(2,1)S(1)}, bf16[16,1024]{1,0:T(8,128)(2,1)S(1)}, u32[]{:S(2)}, u32[]{:S(2)}) collective-permute-start(bf16[16,1024]{1,0:T(8,128)(2,1)S(1)} %get-tuple-element.32), channel_id=1, source_target_pairs={{0,3},{1,0},{2,1},{3,2},{4,7},{5,4},{6,5},{7,6},{8,11},{9,8},{10,9... | collective-permute-start | bytes 98312 | tf_op jit(solution)/shard_map/ppermute | solution.py:407
  51.3 0.4 collective-permute-done
  51.7 0.7 %collective-permute-done.1 = bf16[16,1024]{1,0:T(8,128)(2,1)S(1)} collective-permute-done((bf16[16,1024]{1,0:T(8,128)(2,1)S(1)}, bf16[16,1024]{1,0:T(8,128)(2,1)S(1)}, u32[]{:S(2)}, u32[]{:S(2)}) %collective-permute-start.1) | collective-permute-done | bytes 32800 | tf_op jit(solution)/shard_map/ppermute | solution.py:407
  52.4 0.5 %collective-permute-done.2 = bf16[16,1024]{1,0:T(8,128)(2,1)S(1)} collective-permute-done((bf16[16,1024]{1,0:T(8,128)(2,1)S(1)}, bf16[16,1024]{1,0:T(8,128)(2,1)S(1)}, u32[]{:S(2)}, u32[]{:S(2)}) %collective-permute-start.2) | collective-permute-done | bytes 32800 | tf_op jit(solution)/shard_map/ppermute | solution.py:407
  52.9 0.6 %add_convert_fusion = bf16[16,1024]{1,0:T(8,128)(2,1)} fusion(bf16[16,1024]{1,0:T(8,128)(2,1)S(1)} %collective-permute-done.2, bf16[16,1024]{1,0:T(8,128)(2,1)S(1)} %collective-permute-done.1, bf16[16,1024]{1,0:T(8,128)(2,1)S(1)} %collective-permute-done, bf16[16,1024]{1,0:T(8,128)(2,1)S(1)} %get-tuple-element.29), kind=kLoop, calls=%fused_computation | loop fusion | flops 131072 | bytes 163840 | tf_op jit(solution)/shard_map/convert_element_type | solution.py:408
  (7 shorter events, 0.0 us)
Async XLA Ops:
  1.5 16.2 %all-to-all-start = ((bf16[8,128,128]{2,1,0:T(8,128)(2,1)}), bf16[8,128,128]{2,1,0:T(8,128)(2,1)S(1)}, u32[]{:S(2)}, u32[]{:S(2)}) async-start(bf16[8,128,128]{2,1,0:T(8,128)(2,1)} %broadcast_in_dim.2), calls=%async_computation | async-start | bytes 524288 | tf_op jit(solution)/shard_map/all_to_all | solution.py:329
  9.4 37.5 %copy-start.1 = (s32[2]{0:T(128)S(1)}, s32[2]{0:T(128)}, u32[]{:S(2)}) copy-start(s32[2]{0:T(128)} %pad_add_fusion.own) | copy-start | bytes 28
  14.2 21.9 %copy-start.2 = (s32[48]{0:T(128)S(1)}, s32[48]{0:T(128)}, u32[]{:S(2)}) copy-start(s32[48]{0:T(128)} %get-tuple-element.19.entry_item) | copy-start | bytes 580
  14.2 21.9 %copy-start.3 = (s32[48]{0:T(128)S(1)}, s32[48]{0:T(128)}, u32[]{:S(2)}) copy-start(s32[48]{0:T(128)} %get-tuple-element.20.entry_ok) | copy-start | bytes 580
  17.7 29.2 %copy-start = (bf16[2048,1024]{1,0:T(8,128)(2,1)S(1)}, bf16[2048,1024]{1,0:T(8,128)(2,1)}, u32[]{:S(2)}) copy-start(bf16[2048,1024]{1,0:T(8,128)(2,1)} %weight.1) | copy-start | bytes 12582916
  17.7 0.8 %copy-start.4 = (s32[64]{0:T(128)S(1)}, s32[64]{0:T(128)}, u32[]{:S(2)}) copy-start(s32[64]{0:T(128)} %get-tuple-element.21.item_sequence) | copy-start | bytes 772
  18.5 0.8 %copy-start.5 = (s32[64]{0:T(128)S(1)}, s32[64]{0:T(128)}, u32[]{:S(2)}) copy-start(s32[64]{0:T(128)} %get-tuple-element.22.item_tokens) | copy-start | bytes 772
  19.3 0.7 %copy-start.6 = (s32[64]{0:T(128)S(1)}, s32[64]{0:T(128)}, u32[]{:S(2)}) copy-start(s32[64]{0:T(128)} %get-tuple-element.23.item_list) | copy-start | bytes 772
  48.3 3.4 %collective-permute-start = (bf16[16,1024]{1,0:T(8,128)(2,1)S(1)}, bf16[16,1024]{1,0:T(8,128)(2,1)S(1)}, u32[]{:S(2)}, u32[]{:S(2)}) collective-permute-start(bf16[16,1024]{1,0:T(8,128)(2,1)S(1)} %get-tuple-element.30), channel_id=1, source_target_pairs={{0,1},{1,2},{2,3},{3,0},{4,5},{5,6},{6,7},{7,4},{8,9},{9,10},{10,1... | collective-permute-start | bytes 98312 | tf_op jit(solution)/shard_map/ppermute | solution.py:407
  48.4 4.0 %collective-permute-start.1 = (bf16[16,1024]{1,0:T(8,128)(2,1)S(1)}, bf16[16,1024]{1,0:T(8,128)(2,1)S(1)}, u32[]{:S(2)}, u32[]{:S(2)}) collective-permute-start(bf16[16,1024]{1,0:T(8,128)(2,1)S(1)} %get-tuple-element.31), channel_id=1, source_target_pairs={{0,2},{1,3},{2,0},{3,1},{4,6},{5,7},{6,4},{7,5},{8,10},{9,11},{10,... | collective-permute-start | bytes 98312 | tf_op jit(solution)/shard_map/ppermute | solution.py:407
  49.9 3.0 %collective-permute-start.2 = (bf16[16,1024]{1,0:T(8,128)(2,1)S(1)}, bf16[16,1024]{1,0:T(8,128)(2,1)S(1)}, u32[]{:S(2)}, u32[]{:S(2)}) collective-permute-start(bf16[16,1024]{1,0:T(8,128)(2,1)S(1)} %get-tuple-element.32), channel_id=1, source_target_pairs={{0,3},{1,0},{2,1},{3,2},{4,7},{5,4},{6,5},{7,6},{8,11},{9,8},{10,9... | collective-permute-start | bytes 98312 | tf_op jit(solution)/shard_map/ppermute | solution.py:407

commit v4 on v3

--- a/solution.py
+++ b/solution.py
@@ -15,6 +15,7 @@
 pad_heads = 16
 stat_lanes = 16
 batch = 8
+early_bytes = 5 << 19
 
 
 def three_terms(value):
@@ -87,6 +88,10 @@
     return pltpu.with_memory_space_constraint(array, pltpu.VMEM)
 
 
+def table_of(array):
+    return pltpu.with_memory_space_constraint(array, pltpu.SMEM)
+
+
 def far(array):
     return pltpu.with_memory_space_constraint(array, pltpu.HBM)
 
@@ -100,10 +105,10 @@
     head_parts = mesh.shape["mp"]
 
     def home_kernel(
-        routes, lengths, own, queries, key_up, value_up, resident_far,
+        routes, lengths, queries, key_up, value_up, resident_far, overflow,
         item_sequence, item_tokens, item_list, item_count, entry_item, entry_ok,
-        packed_out, lse_out, blocks, key_near,
-        table, counts, holder_counts, resident, home_sem,
+        packed_out, lse_out, blocks, key_near, pages,
+        table, counts, holder_counts, resident, home_sem, sems,
     ):
         seq_dev, rows, _ = resident.shape
         home_copy = pltpu.make_async_copy(resident_far, resident, home_sem)
@@ -114,7 +119,7 @@
         tail_pages = routes.shape[0]
         home_tokens = rows // kv_heads
         page = lanes
-        me = own[0]
+        me = lax.axis_index("dp")
 
         def scan_group(group, _):
             count = jnp.int32(0)
@@ -144,7 +149,24 @@
                 found = found + (tokens > 0).astype(jnp.int32)
             return found
 
-        item_count[0] = lax.fori_loop(0, group_count, finish_group, jnp.int32(0))
+        found_count = lax.fori_loop(0, group_count, finish_group, jnp.int32(0))
+        item_count[0] = found_count
+
+        def page_copy(place):
+            return pltpu.make_async_copy(
+                overflow.at[item_list[place]], pages.at[place], sems.at[place]
+            )
+
+        def start_copy(place, _):
+            page_copy(place).start()
+            return 0
+
+        def end_copy(place, _):
+            page_copy(place).wait()
+            return 0
+
+        early_count = jnp.minimum(found_count, pages.shape[0])
+        lax.fori_loop(0, early_count, start_copy, 0)
 
         def own_row(row, _):
             length = lengths[me * seq_dev + row]
@@ -177,42 +199,41 @@
             for place, row in enumerate(part):
                 packed_out[row] = packed[place]
                 lse_out[row] = jnp.broadcast_to(lse[place], (pad_heads, lanes))
+        lax.fori_loop(0, early_count, end_copy, 0)
 
     def page_kernel(
-        item_sequence, item_tokens, item_list, item_count, queries, key_up, overflow,
-        out, pages, terms_ref, stats_ref, sems,
+        item_sequence, item_tokens, item_list, item_count, queries, key_up, pages, overflow,
+        out, terms_ref, stats_ref, *late,
     ):
-        items, rows, _ = overflow.shape
+        early, rows, _ = pages.shape
+        items = overflow.shape[0]
         slots = items // group_count
         kv_heads = key_up.shape[0] // half
         found = item_count[0]
 
-        def copy_of(place):
+        def late_copy(place):
+            late_pages, sems = late
             return pltpu.make_async_copy(
-                overflow.at[item_list[place]], pages.at[place], sems.at[place]
+                overflow.at[item_list[place]], late_pages.at[place - early], sems.at[place - early]
             )
 
         def start_copy(place, _):
-            copy_of(place).start()
-            return 0
-
-        lax.fori_loop(0, found, start_copy, 0)
+            late_copy(place).start()
+            return 0
+
+        if late:
+            lax.fori_loop(early, found, start_copy, 0)
         terms_ref[...] = absorbed_queries(queries[...], key_up[...], kv_heads)
         token, head_ok = row_masks(rows, kv_heads)
         stat_lane = lax.broadcasted_iota(jnp.int32, (pad_heads, lanes), 1)
 
-        def one_batch(step, _):
+        def one_batch(step, source, shift):
             first = step * batch
-            for offset in range(batch):
-                @pl.when(first + offset < found)
-                def _():
-                    copy_of(first + offset).wait()
-
             places = [jnp.minimum(first + offset, found - 1) for offset in range(batch)]
             chosen = [item_list[place] for place in places]
             packed, lse = attend_all(
                 [terms_ref[item_sequence[item]] for item in chosen],
-                [pages[place] for place in places],
+                [source[place - shift] for place in places],
                 [head_ok & (token < item_tokens[item]) for item in chosen],
             )
             for offset, item in enumerate(chosen):
@@ -224,9 +245,24 @@
                     mine = stat_lane == slot * stat_lanes + place
                     stats = jnp.where(mine, term.astype(f32), stats)
                 stats_ref[group] = stats
-            return 0
-
-        lax.fori_loop(0, (found + batch - 1) // batch, one_batch, 0)
+
+        def early_batch(step, _):
+            one_batch(step, pages, 0)
+            return 0
+
+        def late_batch(step, _):
+            for offset in range(batch):
+                @pl.when(step * batch + offset < found)
+                def _():
+                    late_copy(step * batch + offset).wait()
+
+            one_batch(step, late[0], early)
+            return 0
+
+        steps = (found + batch - 1) // batch
+        lax.fori_loop(0, jnp.minimum(steps, early // batch), early_batch, 0)
+        if late:
+            lax.fori_loop(early // batch, steps, late_batch, 0)
         out[:, slots] = stats_ref[:, 0:8].astype(bf16)
         out[:, slots + 1] = stats_ref[:, 8:16].astype(bf16)
 
@@ -274,8 +310,9 @@
             for target in range(group_count):
                 out[target, query] = block
 
-    def project_kernel(own, received, value_up, weight, *rest):
+    def project_kernel(received, value_up, weight, *rest):
         outs, out = rest[:head_parts], rest[head_parts]
+        me = lax.axis_index("mp")
         sequences = received.shape[0] * received.shape[2]
         kv_heads = value_up.shape[1] // lanes
         pieces = [
@@ -300,7 +337,7 @@
         result = jnp.dot(both, weight[...], preferred_element_type=f32)
         out[...] = (result[:sequences] + result[sequences:]).astype(bf16).reshape(out.shape)
         for step in range(head_parts):
-            outs[step][...] = out[(own[1] + step) % head_parts]
+            outs[step][...] = out[(me + step) % head_parts]
 
     def body(
         queries, resident_cache, overflow_cache, key_up_weight, value_up_weight,
@@ -317,8 +354,7 @@
         vmem = pl.BlockSpec(memory_space=pltpu.VMEM)
         hbm = pl.BlockSpec(memory_space=pltpu.HBM)
         small = pltpu.CompilerParams(vmem_limit_bytes=16 << 20)
-        ints = lambda size: jax.ShapeDtypeStruct((size,), jnp.int32)
-        own = jnp.stack([lax.axis_index("dp"), lax.axis_index("mp")]).astype(jnp.int32)
+        ints = lambda size: pltpu.SMEM((size,), jnp.int32)
         flat_routes = routes.transpose(1, 2, 0)
         key_up = key_up_weight.reshape(kv_heads * width, head_size)
         flat_queries = queries.reshape(seq_dev * head_dev, head_size)
@@ -331,9 +367,11 @@
         ).reshape(-1, head_size)
 
         entries = seq_dev * tail_pages
+        early = early_bytes // (page * kv_heads * lanes * 2) // batch * batch
+        early = min(-(-items // batch) * batch, early)
         (
             item_sequence, item_tokens, item_list, item_count, entry_item, entry_ok,
-            packed_home, lse_home, blocks, key_near,
+            packed_home, lse_home, blocks, key_near, pages,
         ) = pl.pallas_call(
             home_kernel,
             out_shape=(
@@ -342,39 +380,48 @@
                 near((seq_dev, pad_heads, lanes), f32),
                 near((lanes, kv_heads * head_size), bf16),
                 near(key_up.shape, bf16),
+                near((early, page * kv_heads, lanes), bf16),
             ),
-            in_specs=[smem, smem, smem, vmem, vmem, vmem, hbm],
-            out_specs=(smem,) * 6 + (vmem,) * 4,
+            in_specs=[smem, smem, vmem, vmem, vmem, hbm, hbm],
+            out_specs=(smem,) * 6 + (vmem,) * 5,
             scratch_shapes=[
                 pltpu.SMEM((items + 8,), jnp.int32),
                 pltpu.SMEM((group_count,), jnp.int32),
                 pltpu.SMEM((group_count,), jnp.int32),
                 pltpu.VMEM((seq_dev, home_tokens * kv_heads, lanes), bf16),
                 pltpu.SemaphoreType.DMA,
+                pltpu.SemaphoreType.DMA((early,)),
             ],
+            compiler_params=small,
             cost_estimate=pl.CostEstimate(
                 flops=200_000_000, transcendentals=0, bytes_accessed=1 << 20
             ),
         )(
-            flat_routes, lengths, own, flat_queries, key_up, value_up_weight,
-            resident_cache.reshape(seq_dev, home_tokens * kv_heads, lanes),
+            far(flat_routes), far(lengths), far(flat_queries), far(key_up),
+            far(value_up_weight),
+            far(resident_cache.reshape(seq_dev, home_tokens * kv_heads, lanes)),
+            far(overflow_cache.reshape(items, page * kv_heads, lanes)),
         )
 
+        late = items - early
+        late_scratch = [] if late <= 0 else [
+            pltpu.VMEM((late, page * kv_heads, lanes), bf16),
+            pltpu.SemaphoreType.DMA((late,)),
+        ]
         partials = pl.pallas_call(
             page_kernel,
             out_shape=near((group_count, slots + 2, 8, lanes), bf16),
-            in_specs=[smem, smem, smem, smem, vmem, vmem, hbm],
+            in_specs=[smem, smem, smem, smem, vmem, vmem, vmem, hbm],
             out_specs=vmem,
             scratch_shapes=[
-                pltpu.VMEM((items, page * kv_heads, lanes), bf16),
                 pltpu.VMEM((group_count * seq_dev, 48, lanes), bf16),
                 pltpu.VMEM((group_count, pad_heads, lanes), f32),
-                pltpu.SemaphoreType.DMA((items,)),
-            ],
+            ] + late_scratch,
             compiler_params=small,
         )(
-            item_sequence, item_tokens, item_list, item_count, pin(all_queries), pin(key_near),
-            far(overflow_cache.reshape(items, page * kv_heads, lanes)),
+            table_of(item_sequence), table_of(item_tokens), table_of(item_list),
+            table_of(item_count), pin(all_queries), pin(key_near),
+            pin(pages), far(overflow_cache.reshape(items, page * kv_heads, lanes)),
         )
         partials = lax.all_to_all(partials, "dp", split_axis=0, concat_axis=0, tiled=True)
 
@@ -385,7 +432,7 @@
             out_specs=vmem,
             scratch_shapes=[pltpu.VMEM((seq_dev * 8, lanes), f32)],
             compiler_params=small,
-        )(entry_item, entry_ok, pin(partials), pin(packed_home), pin(lse_home))
+        )(table_of(entry_item), table_of(entry_ok), pin(partials), pin(packed_home), pin(lse_home))
         merged = lax.all_to_all(merged, "dp", split_axis=0, concat_axis=0, tiled=True)
 
         sequences = group_count * seq_dev
@@ -394,13 +441,13 @@
         pieces = pl.pallas_call(
             project_kernel,
             out_shape=(near(piece, bf16),) * head_parts,
-            in_specs=[smem, vmem, vmem, vmem],
+            in_specs=[vmem, vmem, vmem],
             out_specs=(vmem,) * head_parts,
             scratch_shapes=[
                 pltpu.VMEM((head_parts,) + piece, bf16),
             ],
             compiler_params=small,
-        )(own, pin(merged), pin(blocks), out_weight)
+        )(pin(merged), pin(blocks), out_weight)
         total = pieces[0].astype(f32)
         for step in range(1, head_parts):
             ring = [(source, (source + step) % head_parts) for source in range(head_parts)]

time: 54.2 us -> 49.5 us (0.913)
  Pallas kernels: 13.1 us -> 8.65 us
  blocking collectives: 20.1 us -> 22.5 us
  local copies, waits for them, and re-layouts: 3.79 us -> 1.49 us
  other arithmetic: 1.24 us -> 0.63 us
    pallas_call x1, Pallas kernels: 5.81 us -> 2.38 us  [body(): pl.pallas_call(page_kernel, out_shape=near((group_count, slots + 2, 8, la...]
    all_to_all x1, blocking collectives: 10.3 us -> 12.8 us  [body(): lax.all_to_all(partials, 'dp', split_axis=0, concat_axis=0, tiled=True)]
    unnamed x14 -> x2, local copies, waits for them, and re-layouts: 2.31 us -> 0.01 us
    another operation x1 -> x0, other arithmetic: 0.61 us -> none  [body(): jnp.stack([lax.axis_index('dp'), lax.axis_index('mp')]).astype(jnp.int32)]
    pallas_call x1, Pallas kernels: 1.4 us -> 0.85 us  [body(): pl.pallas_call(project_kernel, out_shape=(near(piece, bf16),) * head_part...]
  transfers between devices with their start and end apart: 4 -> 4, of which waited for: 4 -> 4; matrix products, arithmetic and copies ran while one was open for 1% -> 0% of each run, Pallas kernels for 9% -> 10%
where the time goes in v4:
time: 49.5 us; the launch traced here: 49.2 us
  blocking collectives  22.5 us (45%)
  starting transfers between devices  10.3 us (21%)
  Pallas kernels  8.65 us (17%)
  waiting for transfers between devices  5.58 us (11%)
  local copies, waits for them, and re-layouts  1.49 us (3%)
  other arithmetic  0.63 us (1%)
    all_to_all x1, blocking collectives, body(): lax.all_to_all(partials, 'dp', split_axis=0, concat_axis=0, tiled=True)  12.8 us
    all_to_all x1, blocking collectives, body(): lax.all_to_all(merged, 'dp', split_axis=0, concat_axis=0, tiled=True)  9.74 us
    all_to_all x1, starting transfers between devices, body(): lax.all_to_all(spread_queries, 'dp', split_axis=0, concat_axis=0, tiled=T...  7.31 us
    pallas_call x1, Pallas kernels, body(): pl.pallas_call(home_kernel, out_shape=(ints(items), ints(items), ints(ite...  4.93 us
    all_to_all x1, waiting for transfers between devices, body(): lax.all_to_all(spread_queries, 'dp', split_axis=0, concat_axis=0, tiled=T...  3.98 us
    ppermute x3, starting transfers between devices, body(): total = total + lax.ppermute(pieces[step], 'mp', ring).astype(f32)  3.01 us
    pallas_call x1, Pallas kernels, body(): pl.pallas_call(page_kernel, out_shape=near((group_count, slots + 2, 8, la...  2.38 us
    ppermute x3, waiting for transfers between devices, body(): total = total + lax.ppermute(pieces[step], 'mp', ring).astype(f32)  1.6 us
  transfers between devices with their start and end apart: 4, of which 4 were waited for; matrix products, arithmetic and copies ran while one was open for 0% of the time, Pallas kernels for 10%

profile of v4, /device:TPU:0, one launch (start us, length us, event | category | flops | bytes accessed | tf_op | source)
XLA Modules:
  0.0 49.2 jit_solution(2282766712429477234)
XLA Ops:
  0.0 1.5 %broadcast_in_dim.2 = bf16[8,128,128]{2,1,0:T(8,128)(2,1)} broadcast(bf16[128,128]{1,0:T(8,128)(2,1)} %bitcast.10), dimensions={1,2} | broadcast | bytes 294912 | tf_op jit(solution)/shard_map/broadcast_in_dim | solution.py:362
  1.5 7.3 %all-to-all-start = ((bf16[8,128,128]{2,1,0:T(8,128)(2,1)}), bf16[8,128,128]{2,1,0:T(8,128)(2,1)S(1)}, u32[]{:S(2)}, u32[]{:S(2)}) async-start(bf16[8,128,128]{2,1,0:T(8,128)(2,1)} %broadcast_in_dim.2), calls=%async_computation | async-start | bytes 524288 | tf_op jit(solution)/shard_map/all_to_all | solution.py:365
  8.8 4.9 %shard_map.82 = (s32[64]{0:T(128)S(4)}, s32[64]{0:T(128)S(4)}, s32[64]{0:T(128)S(4)}, s32[1]{0:T(128)S(4)}, s32[48]{0:T(128)S(4)}, /*index=5*/s32[48]{0:T(128)S(...) custom-call(s32[6,1,64]{2,1,0:T(1,128)} %bitcast.13, ...), custom_call_target="tpu_custom_call" | custom-call | flops 200000000 | bytes 1048576 | tf_op jit(solution)/shard_map/pallas_call | solution.py:375
  13.7 4.0 %all-to-all-done = bf16[8,128,128]{2,1,0:T(8,128)(2,1)S(1)} async-done(((bf16[8,128,128]{2,1,0:T(8,128)(2,1)}), bf16[8,128,128]{2,1,0:T(8,128)(2,1)S(1)}, u32[]{:S(2)}, u32[]{:S(2)}) %all-to-all-start) | async-done | bytes 262176 | tf_op jit(solution)/shard_map/all_to_all | solution.py:365
  17.7 0.0 copy-start
  17.7 2.4 %shard_map.83 = bf16[8,10,8,128]{3,2,1,0:T(8,128)(2,1)S(1)} custom-call(s32[64]{0:T(128)S(4)} %get-tuple-element.22.item_sequence, s32[64]{0:T(128)S(4)} %get-tuple-element.23.item_tokens, s32[64]{0:T(128)S(4)} %get-tuple-element.24.item_list, s32[1]{0:T(128)S(4)} %get-tuple-element.25.item_count, bf16[1024,128]{1,0:T(8,128)(2,1)S(1)} %bitcast.6, ...), custom_call_target="tpu_custom_call" | custom-call | tf_op jit(solution)/shard_map/pallas_call | solution.py:411
  20.1 12.8 %all_to_all.15.received = bf16[8,10,8,128]{3,2,1,0:T(8,128)(2,1)S(1)} all-to-all(bf16[8,10,8,128]{3,2,1,0:T(8,128)(2,1)S(1)} %shard_map.83), channel_id=1, replica_groups=mesh['dp'=8,'mp'=4] {'dp'}, dimensions={0} | all-to-all | bytes 327680 | tf_op jit(solution)/shard_map/all_to_all | solution.py:426
  32.9 0.5 %shard_map.84 = bf16[8,8,8,128]{3,2,1,0:T(8,128)(2,1)S(1)} custom-call(s32[48]{0:T(128)S(4)} %get-tuple-element.20.entry_item, s32[48]{0:T(128)S(4)} %get-tuple-element.21.entry_ok, bf16[8,10,8,128]{3,2,1,0:T(8,128)(2,1)S(1)} %all_to_all.15.received, f32[8,8,128]{2,1,0:T(8,128)S(1)} %get-tuple-element.28.packed_home, ...), custom_call_target="tpu_custom_call" | custom-call | tf_op jit(solution)/shard_map/pallas_call | solution.py:428
  33.4 9.7 %all_to_all.16.received = bf16[8,8,8,128]{3,2,1,0:T(8,128)(2,1)S(1)} all-to-all(bf16[8,8,8,128]{3,2,1,0:T(8,128)(2,1)S(1)} %shard_map.84), channel_id=1, replica_groups=mesh['dp'=8,'mp'=4] {'dp'}, dimensions={0} | all-to-all | bytes 262144 | tf_op jit(solution)/shard_map/all_to_all | solution.py:436
  43.1 0.0 copy-done
  43.1 0.8 %shard_map.85 = (bf16[16,1024]{1,0:T(8,128)(2,1)S(1)}, bf16[16,1024]{1,0:T(8,128)(2,1)S(1)}, bf16[16,1024]{1,0:T(8,128)(2,1)S(1)}, bf16[16,1024]{1,0:T(8,128)(2,1)S(1)}) custom-call(bf16[8,8,8,128]{3,2,1,0:T(8,128)(2,1)S(1)} %all_to_all.16.received, bf16[128,256]{1,0:T(8,128)(2,1)S(1)} %get-tuple-element.30.value_up, bf16[2048,1024]{1,0:T(8,128)(2,1)S(1)} %copy-done), custom_call_target="tpu_custom_call" | custom-call | tf_op jit(solution)/shard_map/pallas_call | solution.py:441
  44.0 0.1 collective-permute-start
  44.0 1.6 %collective-permute-start.1 = (bf16[16,1024]{1,0:T(8,128)(2,1)S(1)}, bf16[16,1024]{1,0:T(8,128)(2,1)S(1)}, u32[]{:S(2)}, u32[]{:S(2)}) collective-permute-start(bf16[16,1024]{1,0:T(8,128)(2,1)S(1)} %get-tuple-element.33), channel_id=1, source_target_pairs={{0,2},{1,3},{2,0},{3,1},{4,6},{5,7},{6,4},{7,5},{8,10},{9,11},{10,... | collective-permute-start | bytes 98312 | tf_op jit(solution)/shard_map/ppermute | solution.py:454
  45.6 1.4 %collective-permute-start.2 = (bf16[16,1024]{1,0:T(8,128)(2,1)S(1)}, bf16[16,1024]{1,0:T(8,128)(2,1)S(1)}, u32[]{:S(2)}, u32[]{:S(2)}) collective-permute-start(bf16[16,1024]{1,0:T(8,128)(2,1)S(1)} %get-tuple-element.34), channel_id=1, source_target_pairs={{0,3},{1,0},{2,1},{3,2},{4,7},{5,4},{6,5},{7,6},{8,11},{9,8},{10,9... | collective-permute-start | bytes 98312 | tf_op jit(solution)/shard_map/ppermute | solution.py:454
  47.0 0.4 collective-permute-done
  47.4 0.7 %collective-permute-done.1 = bf16[16,1024]{1,0:T(8,128)(2,1)S(1)} collective-permute-done((bf16[16,1024]{1,0:T(8,128)(2,1)S(1)}, bf16[16,1024]{1,0:T(8,128)(2,1)S(1)}, u32[]{:S(2)}, u32[]{:S(2)}) %collective-permute-start.1) | collective-permute-done | bytes 32800 | tf_op jit(solution)/shard_map/ppermute | solution.py:454
  48.0 0.6 %collective-permute-done.2 = bf16[16,1024]{1,0:T(8,128)(2,1)S(1)} collective-permute-done((bf16[16,1024]{1,0:T(8,128)(2,1)S(1)}, bf16[16,1024]{1,0:T(8,128)(2,1)S(1)}, u32[]{:S(2)}, u32[]{:S(2)}) %collective-permute-start.2) | collective-permute-done | bytes 32800 | tf_op jit(solution)/shard_map/ppermute | solution.py:454
  48.6 0.6 %add_convert_fusion = bf16[16,1024]{1,0:T(8,128)(2,1)} fusion(bf16[16,1024]{1,0:T(8,128)(2,1)S(1)} %collective-permute-done.2, bf16[16,1024]{1,0:T(8,128)(2,1)S(1)} %collective-permute-done.1, bf16[16,1024]{1,0:T(8,128)(2,1)S(1)} %collective-permute-done, bf16[16,1024]{1,0:T(8,128)(2,1)S(1)} %get-tuple-element.31), kind=kLoop, calls=%fused_computation | loop fusion | flops 131072 | bytes 163840 | tf_op jit(solution)/shard_map/convert_element_type | solution.py:455
Async XLA Ops:
  1.5 16.2 %all-to-all-start = ((bf16[8,128,128]{2,1,0:T(8,128)(2,1)}), bf16[8,128,128]{2,1,0:T(8,128)(2,1)S(1)}, u32[]{:S(2)}, u32[]{:S(2)}) async-start(bf16[8,128,128]{2,1,0:T(8,128)(2,1)} %broadcast_in_dim.2), calls=%async_computation | async-start | bytes 524288 | tf_op jit(solution)/shard_map/all_to_all | solution.py:365
  17.7 25.4 %copy-start = (bf16[2048,1024]{1,0:T(8,128)(2,1)S(1)}, bf16[2048,1024]{1,0:T(8,128)(2,1)}, u32[]{:S(2)}) copy-start(bf16[2048,1024]{1,0:T(8,128)(2,1)} %weight.1) | copy-start | bytes 12582916
  44.0 3.4 %collective-permute-start = (bf16[16,1024]{1,0:T(8,128)(2,1)S(1)}, bf16[16,1024]{1,0:T(8,128)(2,1)S(1)}, u32[]{:S(2)}, u32[]{:S(2)}) collective-permute-start(bf16[16,1024]{1,0:T(8,128)(2,1)S(1)} %get-tuple-element.32), channel_id=1, source_target_pairs={{0,1},{1,2},{2,3},{3,0},{4,5},{5,6},{6,7},{7,4},{8,9},{9,10},{10,1... | collective-permute-start | bytes 98312 | tf_op jit(solution)/shard_map/ppermute | solution.py:454
  44.0 4.0 %collective-permute-start.1 = (bf16[16,1024]{1,0:T(8,128)(2,1)S(1)}, bf16[16,1024]{1,0:T(8,128)(2,1)S(1)}, u32[]{:S(2)}, u32[]{:S(2)}) collective-permute-start(bf16[16,1024]{1,0:T(8,128)(2,1)S(1)} %get-tuple-element.33), channel_id=1, source_target_pairs={{0,2},{1,3},{2,0},{3,1},{4,6},{5,7},{6,4},{7,5},{8,10},{9,11},{10,... | collective-permute-start | bytes 98312 | tf_op jit(solution)/shard_map/ppermute | solution.py:454
  45.6 3.0 %collective-permute-start.2 = (bf16[16,1024]{1,0:T(8,128)(2,1)S(1)}, bf16[16,1024]{1,0:T(8,128)(2,1)S(1)}, u32[]{:S(2)}, u32[]{:S(2)}) collective-permute-start(bf16[16,1024]{1,0:T(8,128)(2,1)S(1)} %get-tuple-element.34), channel_id=1, source_target_pairs={{0,3},{1,0},{2,1},{3,2},{4,7},{5,4},{6,5},{7,6},{8,11},{9,8},{10,9... | collective-permute-start | bytes 98312 | tf_op jit(solution)/shard_map/ppermute | solution.py:454

commit v5 on v4

--- a/solution.py
+++ b/solution.py
@@ -14,8 +14,8 @@
 half = 64
 pad_heads = 16
 stat_lanes = 16
-batch = 8
-early_bytes = 5 << 19
+batch = 24
+early_bytes = 3 << 20
 
 
 def three_terms(value):
@@ -46,25 +46,38 @@
 
 
 def attend_all(query_terms, latents, valid):
-    products = [
-        lax.dot_general(terms, latent, (((1,), (1,)), ((), ())), preferred_element_type=f32)
-        for terms, latent in zip(query_terms, latents)
-    ]
-    scores = [
-        jnp.where(ok, product[0:16] + product[16:32] + product[32:48], very_low)
-        for ok, product in zip(valid, products)
-    ]
+    pairs = range(0, len(latents), 2)
+    rows = query_terms[0].shape[0]
+    beside = [jnp.concatenate([latents[at], latents[at + 1]], axis=1) for at in pairs]
+    scores = []
+    for at, latent in zip(pairs, beside):
+        none = jnp.zeros_like(query_terms[at])
+        terms = jnp.concatenate(
+            [
+                jnp.concatenate([query_terms[at], none], axis=1),
+                jnp.concatenate([none, query_terms[at + 1]], axis=1),
+            ],
+            axis=0,
+        )
+        product = lax.dot_general(
+            terms, latent, (((1,), (1,)), ((), ())), preferred_element_type=f32
+        )
+        for one, ok in ((product[:rows], valid[at]), (product[rows:], valid[at + 1])):
+            scores.append(jnp.where(ok, one[0:16] + one[16:32] + one[32:48], very_low))
     peaks = [jnp.max(score, axis=1, keepdims=True) for score in scores]
     weights = [jnp.exp2(score - peak) for score, peak in zip(scores, peaks)]
     split = []
     for weight in weights:
         high = weight.astype(bf16)
         low = (weight - high.astype(f32)).astype(bf16)
-        split.append(jnp.concatenate([high, low], axis=0))
-    sums = [
-        jnp.dot(terms, latent, preferred_element_type=f32)
-        for terms, latent in zip(split, latents)
-    ]
+        split += [high, low]
+    sums = []
+    for at, latent in zip(pairs, beside):
+        both = jnp.dot(
+            jnp.concatenate(split[2 * at : 2 * at + 4], axis=0), latent,
+            preferred_element_type=f32,
+        )
+        sums += [both[:32, :lanes], both[32:, lanes:]]
     totals = [jnp.sum(weight, axis=1, keepdims=True) for weight in weights]
     lane = lax.broadcasted_iota(jnp.int32, (8, lanes), 1)
     packed = []
@@ -76,6 +89,11 @@
     return packed, [peak + jnp.log2(total) for peak, total in zip(peaks, totals)]
 
 
+def spread(value):
+    lane = lax.broadcasted_iota(jnp.int32, (8, lanes), 1)
+    return jnp.where(lane < half, value[0:8], value[8:16])
+
+
 def row_masks(rows, kv_heads):
     column = lax.broadcasted_iota(jnp.int32, (pad_heads, rows), 1)
     head = lax.broadcasted_iota(jnp.int32, (pad_heads, rows), 0) // 8
@@ -103,6 +121,10 @@
 def solution(mesh):
     group_count = mesh.shape["dp"]
     head_parts = mesh.shape["mp"]
+
+    def partner(source, step):
+        paired = head_parts & (head_parts - 1) == 0
+        return source ^ step if paired else (source + step) % head_parts
 
     def home_kernel(
         routes, lengths, queries, key_up, value_up, resident_far, overflow,
@@ -198,7 +220,7 @@
             )
             for place, row in enumerate(part):
                 packed_out[row] = packed[place]
-                lse_out[row] = jnp.broadcast_to(lse[place], (pad_heads, lanes))
+                lse_out[row] = spread(lse[place])
         lax.fori_loop(0, early_count, end_copy, 0)
 
     def page_kernel(
@@ -226,6 +248,8 @@
         terms_ref[...] = absorbed_queries(queries[...], key_up[...], kv_heads)
         token, head_ok = row_masks(rows, kv_heads)
         stat_lane = lax.broadcasted_iota(jnp.int32, (pad_heads, lanes), 1)
+        stat_head = lax.broadcasted_iota(jnp.int32, (pad_heads, lanes), 0) // 8
+        stat_lane = stat_lane - stat_head * (stat_lanes // 2)
 
         def one_batch(step, source, shift):
             first = step * batch
@@ -263,21 +287,19 @@
         lax.fori_loop(0, jnp.minimum(steps, early // batch), early_batch, 0)
         if late:
             lax.fori_loop(early // batch, steps, late_batch, 0)
-        out[:, slots] = stats_ref[:, 0:8].astype(bf16)
-        out[:, slots + 1] = stats_ref[:, 8:16].astype(bf16)
+        lane = lax.broadcasted_iota(jnp.int32, (group_count, 8, lanes), 2)
+        stats = jnp.where(
+            lane % stat_lanes < stat_lanes // 2, stats_ref[:, 0:8], stats_ref[:, 8:16]
+        )
+        out[:, slots] = stats.astype(bf16)
 
     def merge_kernel(entry_item, entry_ok, received, packed_home, lse_home, out, rows_ref):
         seq_dev = packed_home.shape[0]
-        slots = received.shape[1] - 2
+        slots = received.shape[1] - 1
         tail_pages = entry_item.shape[0] // seq_dev
-        lane8 = lax.broadcasted_iota(jnp.int32, (8, lanes), 1)
-        lane16 = lax.broadcasted_iota(jnp.int32, (pad_heads, lanes), 1)
-        is_term = (lane16 % stat_lanes) < 3
-        slot_of_lane = lane16 // stat_lanes
-
-        def spread(value):
-            return jnp.where(lane8 < half, value[0:8], value[8:16])
-
+        lane = lax.broadcasted_iota(jnp.int32, (8, lanes), 1)
+        place = lane % stat_lanes
+        slot_of_lane = lane // stat_lanes
         for row in range(seq_dev):
             parts = [(lse_home[row], packed_home[row])]
             for page_index in range(tail_pages):
@@ -285,15 +307,17 @@
                 item = entry_item[entry]
                 holder = item // slots
                 slot = item - holder * slots
-                stats = jnp.concatenate(
-                    [received[holder, slots].astype(f32), received[holder, slots + 1].astype(f32)],
-                    axis=0,
-                )
-                mine = is_term & (slot_of_lane == slot)
-                lse = jnp.sum(jnp.where(mine, stats, 0.0), axis=1, keepdims=True)
-                lse = jnp.where(entry_ok[entry] > 0, lse, very_low)
-                lse = jnp.broadcast_to(lse, (pad_heads, lanes))
-                packed = jnp.where(entry_ok[entry] > 0, received[holder, slot].astype(f32), 0.0)
+                stats = jnp.where(slot_of_lane == slot, received[holder, slots].astype(f32), 0.0)
+                pair = [
+                    jnp.sum(
+                        jnp.where((place >= start) & (place < start + 3), stats, 0.0),
+                        axis=1, keepdims=True,
+                    )
+                    for start in (0, stat_lanes // 2)
+                ]
+                ok = entry_ok[entry] > 0
+                lse = jnp.where(ok, jnp.where(lane < half, pair[0], pair[1]), very_low)
+                packed = jnp.where(ok, received[holder, slot].astype(f32), 0.0)
                 parts.append((lse, packed))
             peak = parts[0][0]
             for lse, _ in parts[1:]:
@@ -301,7 +325,7 @@
             total = jnp.zeros((8, lanes), f32)
             merged = jnp.zeros((8, lanes), f32)
             for lse, packed in parts:
-                factor = spread(jnp.exp2(lse - peak))
+                factor = jnp.exp2(lse - peak)
                 total = total + factor
                 merged = merged + factor * packed
             rows_ref[row * 8 : (row + 1) * 8, :] = merged / total
@@ -337,7 +361,7 @@
         result = jnp.dot(both, weight[...], preferred_element_type=f32)
         out[...] = (result[:sequences] + result[sequences:]).astype(bf16).reshape(out.shape)
         for step in range(head_parts):
-            outs[step][...] = out[(me + step) % head_parts]
+            outs[step][...] = out[partner(me, step)]
 
     def body(
         queries, resident_cache, overflow_cache, key_up_weight, value_up_weight,
@@ -377,7 +401,7 @@
             out_shape=(
                 ints(items), ints(items), ints(items), ints(1), ints(entries), ints(entries),
                 near((seq_dev, 8, lanes), f32),
-                near((seq_dev, pad_heads, lanes), f32),
+                near((seq_dev, 8, lanes), f32),
                 near((lanes, kv_heads * head_size), bf16),
                 near(key_up.shape, bf16),
                 near((early, page * kv_heads, lanes), bf16),
@@ -410,7 +434,7 @@
         ]
         partials = pl.pallas_call(
             page_kernel,
-            out_shape=near((group_count, slots + 2, 8, lanes), bf16),
+            out_shape=near((group_count, slots + 1, 8, lanes), bf16),
             in_specs=[smem, smem, smem, smem, vmem, vmem, vmem, hbm],
             out_specs=vmem,
             scratch_shapes=[
@@ -449,8 +473,8 @@
             compiler_params=small,
         )(pin(merged), pin(blocks), out_weight)
         total = pieces[0].astype(f32)
-        for step in range(1, head_parts):
-            ring = [(source, (source + step) % head_parts) for source in range(head_parts)]
+        for step in reversed(range(1, head_parts)):
+            ring = [(source, partner(source, step)) for source in range(head_parts)]
             total = total + lax.ppermute(pieces[step], "mp", ring).astype(f32)
         return total.astype(bf16)
 

time: 49.5 us -> 46.7 us (0.943); the launches traced: 49.2 us -> 45.9 us
  blocking collectives: 22.5 us -> 19.7 us
  starting transfers between devices: 10.3 us -> 9.23 us
  local copies, waits for them, and re-layouts: 1.49 us -> 2.11 us
    all_to_all x1, blocking collectives: 12.8 us -> 9.94 us  [body(): lax.all_to_all(partials, 'dp', split_axis=0, concat_axis=0, tiled=True)]
    ppermute x3, starting transfers between devices: 3.01 us -> 1.92 us  [body(): total = total + lax.ppermute(pieces[step], 'mp', ring).astype(f32)]
    all_to_all x1, waiting for transfers between devices: 3.98 us -> 3.19 us  [body(): lax.all_to_all(spread_queries, 'dp', split_axis=0, concat_axis=0, tiled=T...]
    unnamed x2 -> x6, local copies, waits for them, and re-layouts: 0.01 us -> 0.62 us
    ppermute x3, waiting for transfers between devices: 1.6 us -> 2.18 us  [body(): total = total + lax.ppermute(pieces[step], 'mp', ring).astype(f32)]
  transfers between devices with their start and end apart: 4 -> 4, of which waited for: 4 -> 3; matrix products, arithmetic and copies ran while one was open for 0% -> 0% of each run, Pallas kernels for 10% -> 11%
where the time goes in v5:
time: 46.7 us; the launch traced here: 45.9 us
  blocking collectives  19.7 us (42%)
  starting transfers between devices  9.23 us (20%)
  Pallas kernels  8.79 us (19%)
  waiting for transfers between devices  5.37 us (11%)
  local copies, waits for them, and re-layouts  2.11 us (5%)
  other arithmetic  0.64 us (1%)
    all_to_all x1, blocking collectives, body(): lax.all_to_all(partials, 'dp', split_axis=0, concat_axis=0, tiled=True)  9.94 us
    all_to_all x1, blocking collectives, body(): lax.all_to_all(merged, 'dp', split_axis=0, concat_axis=0, tiled=True)  9.74 us
    all_to_all x1, starting transfers between devices, body(): lax.all_to_all(spread_queries, 'dp', split_axis=0, concat_axis=0, tiled=T...  7.31 us
    pallas_call x1, Pallas kernels, body(): pl.pallas_call(home_kernel, out_shape=(ints(items), ints(items), ints(ite...  5.1 us
    all_to_all x1, waiting for transfers between devices, body(): lax.all_to_all(spread_queries, 'dp', split_axis=0, concat_axis=0, tiled=T...  3.19 us
    pallas_call x1, Pallas kernels, body(): pl.pallas_call(page_kernel, out_shape=near((group_count, slots + 1, 8, la...  2.38 us
    ppermute x3, waiting for transfers between devices, body(): total = total + lax.ppermute(pieces[step], 'mp', ring).astype(f32)  2.18 us
    ppermute x3, starting transfers between devices, body(): total = total + lax.ppermute(pieces[step], 'mp', ring).astype(f32)  1.92 us
  transfers between devices with their start and end apart: 4, of which 3 were waited for; matrix products, arithmetic and copies ran while one was open for 0% of the time, Pallas kernels for 11%

profile of v5, /device:TPU:0, one launch (start us, length us, event | category | flops | bytes accessed | tf_op | source)
XLA Modules:
  0.0 45.9 jit_solution(7628144195256452813)
XLA Ops:
  0.0 1.5 %broadcast_in_dim.2 = bf16[8,128,128]{2,1,0:T(8,128)(2,1)} broadcast(bf16[128,128]{1,0:T(8,128)(2,1)} %bitcast.10), dimensions={1,2} | broadcast | bytes 294912 | tf_op jit(solution)/shard_map/broadcast_in_dim | solution.py:386
  1.5 7.3 %all-to-all-start = ((bf16[8,128,128]{2,1,0:T(8,128)(2,1)}), bf16[8,128,128]{2,1,0:T(8,128)(2,1)S(1)}, u32[]{:S(2)}, u32[]{:S(2)}) async-start(bf16[8,128,128]{2,1,0:T(8,128)(2,1)} %broadcast_in_dim.2), calls=%async_computation | async-start | bytes 524288 | tf_op jit(solution)/shard_map/all_to_all | solution.py:389
  8.8 5.1 %shard_map.82 = (s32[64]{0:T(128)S(4)}, s32[64]{0:T(128)S(4)}, s32[64]{0:T(128)S(4)}, s32[1]{0:T(128)S(4)}, s32[48]{0:T(128)S(4)}, /*index=5*/s32[48]{0:T(128)S(...) custom-call(s32[6,1,64]{2,1,0:T(1,128)} %bitcast.13, ...), custom_call_target="tpu_custom_call" | custom-call | flops 200000000 | bytes 1048576 | tf_op jit(solution)/shard_map/pallas_call | solution.py:399
  13.9 0.0 copy-start.1
  13.9 0.6 %copy-done.1 = f32[8,8,128]{2,1,0:T(8,128)} copy-done((f32[8,8,128]{2,1,0:T(8,128)}, f32[8,8,128]{2,1,0:T(8,128)S(1)}, u32[]{:S(2)}) %copy-start.1) | copy-done | bytes 32792
  14.5 3.2 %all-to-all-done = bf16[8,128,128]{2,1,0:T(8,128)(2,1)S(1)} async-done(((bf16[8,128,128]{2,1,0:T(8,128)(2,1)}), bf16[8,128,128]{2,1,0:T(8,128)(2,1)S(1)}, u32[]{:S(2)}, u32[]{:S(2)}) %all-to-all-start) | async-done | bytes 262176 | tf_op jit(solution)/shard_map/all_to_all | solution.py:389
  17.7 0.0 copy-start.2
  17.7 0.0 copy-start
  17.7 2.4 %shard_map.83 = bf16[8,9,8,128]{3,2,1,0:T(8,128)(2,1)S(1)} custom-call(s32[64]{0:T(128)S(4)} %get-tuple-element.22.item_sequence, s32[64]{0:T(128)S(4)} %get-tuple-element.23.item_tokens, s32[64]{0:T(128)S(4)} %get-tuple-element.24.item_list, s32[1]{0:T(128)S(4)} %get-tuple-element.25.item_count, bf16[1024,128]{1,0:T(8,128)(2,1)S(1)} %bitcast.6, ...), custom_call_target="tpu_custom_call" | custom-call | tf_op jit(solution)/shard_map/pallas_call | solution.py:435
  20.1 9.9 %all_to_all.15.received = bf16[8,9,8,128]{3,2,1,0:T(8,128)(2,1)S(1)} all-to-all(bf16[8,9,8,128]{3,2,1,0:T(8,128)(2,1)S(1)} %shard_map.83), channel_id=1, replica_groups=mesh['dp'=8,'mp'=4] {'dp'}, dimensions={0} | all-to-all | bytes 294912 | tf_op jit(solution)/shard_map/all_to_all | solution.py:450
  30.1 0.0 copy-done.2
  30.1 0.5 %shard_map.84 = bf16[8,8,8,128]{3,2,1,0:T(8,128)(2,1)S(1)} custom-call(s32[48]{0:T(128)S(4)} %get-tuple-element.20.entry_item, s32[48]{0:T(128)S(4)} %get-tuple-element.21.entry_ok, bf16[8,9,8,128]{3,2,1,0:T(8,128)(2,1)S(1)} %all_to_all.15.received, f32[8,8,128]{2,1,0:T(8,128)S(1)} %get-tuple-element.28.packed_home, f32[8,8,128]{2,1,0:T(8,128)S(1)} %copy-done.2), custom_call_target="tpu_custom_call" | custom-call | tf_op jit(solution)/shard_map/pallas_call | solution.py:452
  30.5 9.7 %all_to_all.16.received = bf16[8,8,8,128]{3,2,1,0:T(8,128)(2,1)S(1)} all-to-all(bf16[8,8,8,128]{3,2,1,0:T(8,128)(2,1)S(1)} %shard_map.84), channel_id=1, replica_groups=mesh['dp'=8,'mp'=4] {'dp'}, dimensions={0} | all-to-all | bytes 262144 | tf_op jit(solution)/shard_map/all_to_all | solution.py:460
  40.3 0.0 copy-done
  40.3 0.8 %shard_map.85 = (bf16[16,1024]{1,0:T(8,128)(2,1)S(1)}, bf16[16,1024]{1,0:T(8,128)(2,1)S(1)}, bf16[16,1024]{1,0:T(8,128)(2,1)S(1)}, bf16[16,1024]{1,0:T(8,128)(2,1)S(1)}) custom-call(bf16[8,8,8,128]{3,2,1,0:T(8,128)(2,1)S(1)} %all_to_all.16.received, bf16[128,256]{1,0:T(8,128)(2,1)S(1)} %get-tuple-element.30.value_up, bf16[2048,1024]{1,0:T(8,128)(2,1)S(1)} %copy-done), custom_call_target="tpu_custom_call" | custom-call | tf_op jit(solution)/shard_map/pallas_call | solution.py:465
  41.1 0.1 collective-permute-start
  41.2 1.6 %collective-permute-start.1 = (bf16[16,1024]{1,0:T(8,128)(2,1)S(1)}, bf16[16,1024]{1,0:T(8,128)(2,1)S(1)}, u32[]{:S(2)}, u32[]{:S(2)}) collective-permute-start(bf16[16,1024]{1,0:T(8,128)(2,1)S(1)} %get-tuple-element.33), channel_id=1, source_target_pairs={{0,2},{1,3},{2,0},{3,1},{4,6},{5,7},{6,4},{7,5},{8,10},{9,11},{10,... | collective-permute-start | bytes 98312 | tf_op jit(solution)/shard_map/ppermute | solution.py:478
  42.7 0.3 collective-permute-start.2
  43.0 1.8 %collective-permute-done = bf16[16,1024]{1,0:T(8,128)(2,1)S(1)} collective-permute-done((bf16[16,1024]{1,0:T(8,128)(2,1)S(1)}, bf16[16,1024]{1,0:T(8,128)(2,1)S(1)}, u32[]{:S(2)}, u32[]{:S(2)}) %collective-permute-start) | collective-permute-done | bytes 32800 | tf_op jit(solution)/shard_map/ppermute | solution.py:478
  44.8 0.4 collective-permute-done.1
  45.2 0.0 collective-permute-done.2
  45.2 0.6 %add_convert_fusion = bf16[16,1024]{1,0:T(8,128)(2,1)} fusion(bf16[16,1024]{1,0:T(8,128)(2,1)S(1)} %collective-permute-done.2, bf16[16,1024]{1,0:T(8,128)(2,1)S(1)} %collective-permute-done.1, bf16[16,1024]{1,0:T(8,128)(2,1)S(1)} %collective-permute-done, bf16[16,1024]{1,0:T(8,128)(2,1)S(1)} %get-tuple-element.31), kind=kLoop, calls=%fused_computation | loop fusion | flops 131072 | bytes 163840 | tf_op jit(solution)/shard_map/convert_element_type | solution.py:479
Async XLA Ops:
  1.5 16.2 %all-to-all-start = ((bf16[8,128,128]{2,1,0:T(8,128)(2,1)}), bf16[8,128,128]{2,1,0:T(8,128)(2,1)S(1)}, u32[]{:S(2)}, u32[]{:S(2)}) async-start(bf16[8,128,128]{2,1,0:T(8,128)(2,1)} %broadcast_in_dim.2), calls=%async_computation | async-start | bytes 524288 | tf_op jit(solution)/shard_map/all_to_all | solution.py:389
  13.9 0.6 %copy-start.1 = (f32[8,8,128]{2,1,0:T(8,128)}, f32[8,8,128]{2,1,0:T(8,128)S(1)}, u32[]{:S(2)}) copy-start(f32[8,8,128]{2,1,0:T(8,128)S(1)} %get-tuple-element.29.lse_home) | copy-start | bytes 98308
  17.7 12.3 %copy-start.2 = (f32[8,8,128]{2,1,0:T(8,128)S(1)}, f32[8,8,128]{2,1,0:T(8,128)}, u32[]{:S(2)}) copy-start(f32[8,8,128]{2,1,0:T(8,128)} %copy-done.1) | copy-start | bytes 98308
  17.7 22.5 %copy-start = (bf16[2048,1024]{1,0:T(8,128)(2,1)S(1)}, bf16[2048,1024]{1,0:T(8,128)(2,1)}, u32[]{:S(2)}) copy-start(bf16[2048,1024]{1,0:T(8,128)(2,1)} %weight.1) | copy-start | bytes 12582916
  41.1 3.7 %collective-permute-start = (bf16[16,1024]{1,0:T(8,128)(2,1)S(1)}, bf16[16,1024]{1,0:T(8,128)(2,1)S(1)}, u32[]{:S(2)}, u32[]{:S(2)}) collective-permute-start(bf16[16,1024]{1,0:T(8,128)(2,1)S(1)} %get-tuple-element.32), channel_id=1, source_target_pairs={{0,3},{1,2},{2,1},{3,0},{4,7},{5,6},{6,5},{7,4},{8,11},{9,10},{10,... | collective-permute-start | bytes 98312 | tf_op jit(solution)/shard_map/ppermute | solution.py:478
  41.2 4.0 %collective-permute-start.1 = (bf16[16,1024]{1,0:T(8,128)(2,1)S(1)}, bf16[16,1024]{1,0:T(8,128)(2,1)S(1)}, u32[]{:S(2)}, u32[]{:S(2)}) collective-permute-start(bf16[16,1024]{1,0:T(8,128)(2,1)S(1)} %get-tuple-element.33), channel_id=1, source_target_pairs={{0,2},{1,3},{2,0},{3,1},{4,6},{5,7},{6,4},{7,5},{8,10},{9,11},{10,... | collective-permute-start | bytes 98312 | tf_op jit(solution)/shard_map/ppermute | solution.py:478
  42.7 2.5 %collective-permute-start.2 = (bf16[16,1024]{1,0:T(8,128)(2,1)S(1)}, bf16[16,1024]{1,0:T(8,128)(2,1)S(1)}, u32[]{:S(2)}, u32[]{:S(2)}) collective-permute-start(bf16[16,1024]{1,0:T(8,128)(2,1)S(1)} %get-tuple-element.34), channel_id=1, source_target_pairs={{0,1},{1,0},{2,3},{3,2},{4,5},{5,4},{6,7},{7,6},{8,9},{9,8},{10,11... | collective-permute-start | bytes 98312 | tf_op jit(solution)/shard_map/ppermute | solution.py:478

commit v6 on v5

--- a/solution.py
+++ b/solution.py
@@ -14,7 +14,10 @@
 half = 64
 pad_heads = 16
 stat_lanes = 16
-batch = 24
+batch = 8
+batches = (24,)
+sequence_unit = 1 << 10
+item_unit = 1 << 22
 early_bytes = 3 << 20
 
 
@@ -128,56 +131,42 @@
 
     def home_kernel(
         routes, lengths, queries, key_up, value_up, resident_far, overflow,
-        item_sequence, item_tokens, item_list, item_count, entry_item, entry_ok,
-        packed_out, lse_out, blocks, key_near, pages,
-        table, counts, holder_counts, resident, home_sem, sems,
+        page_list, page_count, entry_item, entry_ok,
+        packed_out, lse_out, value_near, key_near, pages,
+        holder_counts, resident, home_sem, sems,
     ):
         seq_dev, rows, _ = resident.shape
         home_copy = pltpu.make_async_copy(resident_far, resident, home_sem)
         home_copy.start()
         kv_heads = key_up.shape[0] // half
-        items = item_sequence.shape[0]
+        items = overflow.shape[0]
         slots = items // group_count
         tail_pages = routes.shape[0]
         home_tokens = rows // kv_heads
         page = lanes
         me = lax.axis_index("dp")
 
-        def scan_group(group, _):
-            count = jnp.int32(0)
+        def scan_group(group, found):
+            slot = jnp.int32(0)
+            holder_counts[group] = 0
             for row in range(seq_dev):
+                sequence = group * seq_dev + row
+                length = lengths[sequence]
+                label = group * (slots * item_unit) + sequence * sequence_unit
                 for place in range(tail_pages):
-                    table[group * slots + count] = row * tail_pages + place
-                    named = routes[place, 0, group * seq_dev + row] == me
-                    count = count + named.astype(jnp.int32)
-            counts[group] = count
-            holder_counts[group] = 0
-            return 0
-
-        lax.fori_loop(0, group_count, scan_group, 0)
-
-        def finish_group(group, found):
-            for slot in range(slots):
-                item = group * slots + slot
-                here = slot < counts[group]
-                entry = jnp.where(here, table[item], 0)
-                row = entry // tail_pages
-                sequence = group * seq_dev + row
-                first = home_tokens + (entry - row * tail_pages) * page
-                tokens = jnp.where(here, jnp.clip(lengths[sequence] - first, 0, page), 0)
-                item_sequence[item] = sequence
-                item_tokens[item] = tokens
-                item_list[found] = item
-                found = found + (tokens > 0).astype(jnp.int32)
+                    tokens = jnp.minimum(length - (home_tokens + place * page), page)
+                    named = routes[place, 0, sequence] == me
+                    page_list[found] = slot * item_unit + (label + tokens)
+                    slot = slot + named.astype(jnp.int32)
+                    found = found + (named & (tokens > 0)).astype(jnp.int32)
             return found
 
-        found_count = lax.fori_loop(0, group_count, finish_group, jnp.int32(0))
-        item_count[0] = found_count
+        found_count = lax.fori_loop(0, group_count, scan_group, jnp.int32(0))
+        page_count[0] = found_count
 
         def page_copy(place):
-            return pltpu.make_async_copy(
-                overflow.at[item_list[place]], pages.at[place], sems.at[place]
-            )
+            item = page_list[place] // item_unit
+            return pltpu.make_async_copy(overflow.at[item], pages.at[place], sems.at[place])
 
         def start_copy(place, _):
             page_copy(place).start()
@@ -189,8 +178,8 @@
 
         early_count = jnp.minimum(found_count, pages.shape[0])
         lax.fori_loop(0, early_count, start_copy, 0)
-
-        def own_row(row, _):
+        home_copy.wait()
+        for row in range(seq_dev):
             length = lengths[me * seq_dev + row]
             for place in range(tail_pages):
                 entry = row * tail_pages + place
@@ -199,18 +188,10 @@
                 holder_counts[holder] = slot + 1
                 entry_item[entry] = holder * slots + slot
                 entry_ok[entry] = (home_tokens + place * page < length).astype(jnp.int32)
-            return 0
-
-        lax.fori_loop(0, seq_dev, own_row, 0)
-
         key_near[...] = key_up[...]
-        blocks[...] = jnp.zeros(blocks.shape, bf16)
-        for head in range(kv_heads):
-            across = slice(head * lanes, (head + 1) * lanes)
-            blocks[head * half : (head + 1) * half, across] = value_up[head]
+        value_near[...] = value_up[...]
         terms = absorbed_queries(queries[...], key_up[...], kv_heads)
         token, head_ok = row_masks(rows, kv_heads)
-        home_copy.wait()
         for start in range(0, seq_dev, 4):
             part = range(start, min(start + 4, seq_dev))
             packed, lse = attend_all(
@@ -224,23 +205,27 @@
         lax.fori_loop(0, early_count, end_copy, 0)
 
     def page_kernel(
-        item_sequence, item_tokens, item_list, item_count, queries, key_up, pages, overflow,
+        page_list, page_count, queries, key_up, pages, overflow,
         out, terms_ref, stats_ref, *late,
     ):
         early, rows, _ = pages.shape
         items = overflow.shape[0]
         slots = items // group_count
         kv_heads = key_up.shape[0] // half
-        found = item_count[0]
+        found = page_count[0]
 
         def late_copy(place):
             late_pages, sems = late
-            return pltpu.make_async_copy(
-                overflow.at[item_list[place]], late_pages.at[place - early], sems.at[place - early]
-            )
+            item = page_list[place] // item_unit
+            at = place - early
+            return pltpu.make_async_copy(overflow.at[item], late_pages.at[at], sems.at[at])
 
         def start_copy(place, _):
             late_copy(place).start()
+            return 0
+
+        def end_copy(place, _):
+            late_copy(place).wait()
             return 0
 
         if late:
@@ -251,14 +236,14 @@
         stat_head = lax.broadcasted_iota(jnp.int32, (pad_heads, lanes), 0) // 8
         stat_lane = stat_lane - stat_head * (stat_lanes // 2)
 
-        def one_batch(step, source, shift):
-            first = step * batch
-            places = [jnp.minimum(first + offset, found - 1) for offset in range(batch)]
-            chosen = [item_list[place] for place in places]
+        def one_batch(first, size, source, shift):
+            places = [jnp.minimum(first + offset, found - 1) for offset in range(size)]
+            labels = [page_list[place] for place in places]
+            chosen = [label // item_unit for label in labels]
             packed, lse = attend_all(
-                [terms_ref[item_sequence[item]] for item in chosen],
+                [terms_ref[label % item_unit // sequence_unit] for label in labels],
                 [source[place - shift] for place in places],
-                [head_ok & (token < item_tokens[item]) for item in chosen],
+                [head_ok & (token < label % sequence_unit) for label in labels],
             )
             for offset, item in enumerate(chosen):
                 group = item // slots
@@ -270,23 +255,26 @@
                     stats = jnp.where(mine, term.astype(f32), stats)
                 stats_ref[group] = stats
 
-        def early_batch(step, _):
-            one_batch(step, pages, 0)
+        sizes = sorted({size for size in batches if size < early} | {early})
+        for before, size in zip([0] + sizes, sizes):
+            fits = (found > before) & (found <= size)
+            if size == early:
+                fits = found > before
+
+            @pl.when(fits)
+            def _(size=size):
+                one_batch(0, size, pages, 0)
+
+        def late_batch(step, _):
+            one_batch(early + step * batch, batch, late[0], early)
             return 0
 
-        def late_batch(step, _):
-            for offset in range(batch):
-                @pl.when(step * batch + offset < found)
-                def _():
-                    late_copy(step * batch + offset).wait()
-
-            one_batch(step, late[0], early)
-            return 0
-
-        steps = (found + batch - 1) // batch
-        lax.fori_loop(0, jnp.minimum(steps, early // batch), early_batch, 0)
         if late:
-            lax.fori_loop(early // batch, steps, late_batch, 0)
+            @pl.when(found > early)
+            def _():
+                lax.fori_loop(early, found, end_copy, 0)
+                lax.fori_loop(0, (found - early + batch - 1) // batch, late_batch, 0)
+
         lane = lax.broadcasted_iota(jnp.int32, (group_count, 8, lanes), 2)
         stats = jnp.where(
             lane % stat_lanes < stat_lanes // 2, stats_ref[:, 0:8], stats_ref[:, 8:16]
@@ -338,11 +326,23 @@
         outs, out = rest[:head_parts], rest[head_parts]
         me = lax.axis_index("mp")
         sequences = received.shape[0] * received.shape[2]
-        kv_heads = value_up.shape[1] // lanes
+        kv_heads = value_up.shape[0]
+        blank = jnp.zeros((half, lanes), bf16)
+        blocks = jnp.concatenate(
+            [
+                jnp.concatenate(
+                    [value_up[head] if head == across else blank for across in range(kv_heads)],
+                    axis=1,
+                )
+                for head in range(kv_heads)
+            ]
+            + [jnp.zeros((half, kv_heads * lanes), bf16)] * (2 - kv_heads),
+            axis=0,
+        )
         pieces = [
             jnp.dot(
                 received[:, query].astype(f32).reshape(sequences, lanes).astype(bf16),
-                value_up[...],
+                blocks,
                 preferred_element_type=f32,
             )
             for query in range(8)
@@ -392,25 +392,23 @@
 
         entries = seq_dev * tail_pages
         early = early_bytes // (page * kv_heads * lanes * 2) // batch * batch
-        early = min(-(-items // batch) * batch, early)
+        early = min(items, early)
         (
-            item_sequence, item_tokens, item_list, item_count, entry_item, entry_ok,
-            packed_home, lse_home, blocks, key_near, pages,
+            page_list, page_count, entry_item, entry_ok,
+            packed_home, lse_home, value_near, key_near, pages,
         ) = pl.pallas_call(
             home_kernel,
             out_shape=(
-                ints(items), ints(items), ints(items), ints(1), ints(entries), ints(entries),
+                ints(items + 1), ints(1), ints(entries), ints(entries),
                 near((seq_dev, 8, lanes), f32),
                 near((seq_dev, 8, lanes), f32),
-                near((lanes, kv_heads * head_size), bf16),
+                near(value_up_weight.shape, bf16),
                 near(key_up.shape, bf16),
                 near((early, page * kv_heads, lanes), bf16),
             ),
             in_specs=[smem, smem, vmem, vmem, vmem, hbm, hbm],
-            out_specs=(smem,) * 6 + (vmem,) * 5,
+            out_specs=(smem,) * 4 + (vmem,) * 5,
             scratch_shapes=[
-                pltpu.SMEM((items + 8,), jnp.int32),
-                pltpu.SMEM((group_count,), jnp.int32),
                 pltpu.SMEM((group_count,), jnp.int32),
                 pltpu.VMEM((seq_dev, home_tokens * kv_heads, lanes), bf16),
                 pltpu.SemaphoreType.DMA,
@@ -435,7 +433,7 @@
         partials = pl.pallas_call(
             page_kernel,
             out_shape=near((group_count, slots + 1, 8, lanes), bf16),
-            in_specs=[smem, smem, smem, smem, vmem, vmem, vmem, hbm],
+            in_specs=[smem, smem, vmem, vmem, vmem, hbm],
             out_specs=vmem,
             scratch_shapes=[
                 pltpu.VMEM((group_count * seq_dev, 48, lanes), bf16),
@@ -443,8 +441,7 @@
             ] + late_scratch,
             compiler_params=small,
         )(
-            table_of(item_sequence), table_of(item_tokens), table_of(item_list),
-            table_of(item_count), pin(all_queries), pin(key_near),
+            table_of(page_list), table_of(page_count), pin(all_queries), pin(key_near),
             pin(pages), far(overflow_cache.reshape(items, page * kv_heads, lanes)),
         )
         partials = lax.all_to_all(partials, "dp", split_axis=0, concat_axis=0, tiled=True)
@@ -471,7 +468,7 @@
                 pltpu.VMEM((head_parts,) + piece, bf16),
             ],
             compiler_params=small,
-        )(pin(merged), pin(blocks), out_weight)
+        )(pin(merged), pin(value_near), out_weight)
         total = pieces[0].astype(f32)
         for step in reversed(range(1, head_parts)):
             ring = [(source, partner(source, step)) for source in range(head_parts)]

time: 46.7 us -> 46.3 us (level)
  local copies, waits for them, and re-layouts: 2.11 us -> 1.49 us
  waiting for transfers between devices: 5.37 us -> 5.91 us
    unnamed x6 -> x2, local copies, waits for them, and re-layouts: 0.62 us -> 0.01 us
    all_to_all x1, waiting for transfers between devices: 3.19 us -> 3.73 us  [body(): lax.all_to_all(spread_queries, 'dp', split_axis=0, concat_axis=0, tiled=T...]
where the time goes in v6:
time: 46.3 us; the launch traced here: 45.9 us
  blocking collectives  19.9 us (43%)
  starting transfers between devices  9.23 us (20%)
  Pallas kernels  8.72 us (19%)
  waiting for transfers between devices  5.91 us (13%)
  local copies, waits for them, and re-layouts  1.49 us (3%)
  other arithmetic  0.64 us (1%)
    all_to_all x1, blocking collectives, body(): lax.all_to_all(partials, 'dp', split_axis=0, concat_axis=0, tiled=True)  10.1 us
    all_to_all x1, blocking collectives, body(): lax.all_to_all(merged, 'dp', split_axis=0, concat_axis=0, tiled=True)  9.74 us
    all_to_all x1, starting transfers between devices, body(): lax.all_to_all(spread_queries, 'dp', split_axis=0, concat_axis=0, tiled=T...  7.31 us
    pallas_call x1, Pallas kernels, body(): pl.pallas_call(home_kernel, out_shape=(ints(items + 1), ints(1), ints(ent...  5.18 us
    all_to_all x1, waiting for transfers between devices, body(): lax.all_to_all(spread_queries, 'dp', split_axis=0, concat_axis=0, tiled=T...  3.73 us
    pallas_call x1, Pallas kernels, body(): pl.pallas_call(page_kernel, out_shape=near((group_count, slots + 1, 8, la...  2.23 us
    ppermute x3, waiting for transfers between devices, body(): total = total + lax.ppermute(pieces[step], 'mp', ring).astype(f32)  2.18 us
    ppermute x3, starting transfers between devices, body(): total = total + lax.ppermute(pieces[step], 'mp', ring).astype(f32)  1.92 us
  transfers between devices with their start and end apart: 4, of which 3 were waited for; matrix products, arithmetic and copies ran while one was open for 0% of the time, Pallas kernels for 11%

profile of v6, /device:TPU:0, one launch (start us, length us, event | category | flops | bytes accessed | tf_op | source)
XLA Modules:
  0.0 45.9 jit_solution(13184054728999974323)
XLA Ops:
  0.0 1.5 %broadcast_in_dim.2 = bf16[8,128,128]{2,1,0:T(8,128)(2,1)} broadcast(bf16[128,128]{1,0:T(8,128)(2,1)} %bitcast.10), dimensions={1,2} | broadcast | bytes 294912 | tf_op jit(solution)/shard_map/broadcast_in_dim | solution.py:386
  1.5 7.3 %all-to-all-start = ((bf16[8,128,128]{2,1,0:T(8,128)(2,1)}), bf16[8,128,128]{2,1,0:T(8,128)(2,1)S(1)}, u32[]{:S(2)}, u32[]{:S(2)}) async-start(bf16[8,128,128]{2,1,0:T(8,128)(2,1)} %broadcast_in_dim.2), calls=%async_computation | async-start | bytes 524288 | tf_op jit(solution)/shard_map/all_to_all | solution.py:389
  8.8 5.2 %shard_map.82 = (s32[65]{0:T(128)S(4)}, s32[1]{0:T(128)S(4)}, s32[48]{0:T(128)S(4)}, s32[48]{0:T(128)S(4)}, f32[8,8,128]{2,1,0:T(8,128)S(1)}, /*index=5*/f32[8,8...) custom-call(s32[6,1,64]{2,1,0:T(1,128)} %bitcast.13, ...), custom_call_target="tpu_custom_call" | custom-call | flops 200000000 | bytes 1048576 | tf_op jit(solution)/shard_map/pallas_call | solution.py:399
  14.0 3.7 %all-to-all-done = bf16[8,128,128]{2,1,0:T(8,128)(2,1)S(1)} async-done(((bf16[8,128,128]{2,1,0:T(8,128)(2,1)}), bf16[8,128,128]{2,1,0:T(8,128)(2,1)S(1)}, u32[]{:S(2)}, u32[]{:S(2)}) %all-to-all-start) | async-done | bytes 262176 | tf_op jit(solution)/shard_map/all_to_all | solution.py:389
  17.7 0.0 copy-start
  17.7 2.2 %shard_map.83 = bf16[8,9,8,128]{3,2,1,0:T(8,128)(2,1)S(1)} custom-call(s32[65]{0:T(128)S(4)} %get-tuple-element.20.page_list, s32[1]{0:T(128)S(4)} %get-tuple-element.21.page_count, bf16[1024,128]{1,0:T(8,128)(2,1)S(1)} %bitcast.6, bf16[128,128]{1,0:T(8,128)(2,1)S(1)} %get-tuple-element.22.key_up, bf16[48,256,128]{2,1,0:T(8,128)(2,1)S(1)} %get-tuple-element.23.pages, ...), custom_call_target="tpu_custom_call" | custom-call | tf_op jit(solution)/shard_map/pallas_call | solution.py:433
  20.0 10.1 %all_to_all.15.received = bf16[8,9,8,128]{3,2,1,0:T(8,128)(2,1)S(1)} all-to-all(bf16[8,9,8,128]{3,2,1,0:T(8,128)(2,1)S(1)} %shard_map.83), channel_id=1, replica_groups=mesh['dp'=8,'mp'=4] {'dp'}, dimensions={0} | all-to-all | bytes 294912 | tf_op jit(solution)/shard_map/all_to_all | solution.py:447
  30.1 0.5 %shard_map.84 = bf16[8,8,8,128]{3,2,1,0:T(8,128)(2,1)S(1)} custom-call(s32[48]{0:T(128)S(4)} %get-tuple-element.18.entry_item, s32[48]{0:T(128)S(4)} %get-tuple-element.19.entry_ok, bf16[8,9,8,128]{3,2,1,0:T(8,128)(2,1)S(1)} %all_to_all.15.received, f32[8,8,128]{2,1,0:T(8,128)S(1)} %get-tuple-element.24.packed_home, f32[8,8,128]{2,1,0:T(8,128)S(1)} %get-tuple-element.25.lse_home), custom_call_target="tpu_custom_call" | custom-call | tf_op jit(solution)/shard_map/pallas_call | solution.py:449
  30.5 9.7 %all_to_all.16.received = bf16[8,8,8,128]{3,2,1,0:T(8,128)(2,1)S(1)} all-to-all(bf16[8,8,8,128]{3,2,1,0:T(8,128)(2,1)S(1)} %shard_map.84), channel_id=1, replica_groups=mesh['dp'=8,'mp'=4] {'dp'}, dimensions={0} | all-to-all | bytes 262144 | tf_op jit(solution)/shard_map/all_to_all | solution.py:457
  40.3 0.0 copy-done
  40.3 0.8 %shard_map.85 = (bf16[16,1024]{1,0:T(8,128)(2,1)S(1)}, bf16[16,1024]{1,0:T(8,128)(2,1)S(1)}, bf16[16,1024]{1,0:T(8,128)(2,1)S(1)}, bf16[16,1024]{1,0:T(8,128)(2,1)S(1)}) custom-call(bf16[8,8,8,128]{3,2,1,0:T(8,128)(2,1)S(1)} %all_to_all.16.received, bf16[2,64,128]{2,1,0:T(8,128)(2,1)S(1)} %get-tuple-element.26.value_up, bf16[2048,1024]{1,0:T(8,128)(2,1)S(1)} %copy-done), custom_call_target="tpu_custom_call" | custom-call | tf_op jit(solution)/shard_map/pallas_call | solution.py:462
  41.1 0.1 collective-permute-start
  41.2 1.5 %collective-permute-start.1 = (bf16[16,1024]{1,0:T(8,128)(2,1)S(1)}, bf16[16,1024]{1,0:T(8,128)(2,1)S(1)}, u32[]{:S(2)}, u32[]{:S(2)}) collective-permute-start(bf16[16,1024]{1,0:T(8,128)(2,1)S(1)} %get-tuple-element.29), channel_id=1, source_target_pairs={{0,2},{1,3},{2,0},{3,1},{4,6},{5,7},{6,4},{7,5},{8,10},{9,11},{10,... | collective-permute-start | bytes 98312 | tf_op jit(solution)/shard_map/ppermute | solution.py:475
  42.8 0.3 collective-permute-start.2
  43.1 1.8 %collective-permute-done = bf16[16,1024]{1,0:T(8,128)(2,1)S(1)} collective-permute-done((bf16[16,1024]{1,0:T(8,128)(2,1)S(1)}, bf16[16,1024]{1,0:T(8,128)(2,1)S(1)}, u32[]{:S(2)}, u32[]{:S(2)}) %collective-permute-start) | collective-permute-done | bytes 32800 | tf_op jit(solution)/shard_map/ppermute | solution.py:475
  44.9 0.4 collective-permute-done.1
  45.2 0.0 collective-permute-done.2
  45.2 0.6 %add_convert_fusion = bf16[16,1024]{1,0:T(8,128)(2,1)} fusion(bf16[16,1024]{1,0:T(8,128)(2,1)S(1)} %collective-permute-done.2, bf16[16,1024]{1,0:T(8,128)(2,1)S(1)} %collective-permute-done.1, bf16[16,1024]{1,0:T(8,128)(2,1)S(1)} %collective-permute-done, bf16[16,1024]{1,0:T(8,128)(2,1)S(1)} %get-tuple-element.27), kind=kLoop, calls=%fused_computation | loop fusion | flops 131072 | bytes 163840 | tf_op jit(solution)/shard_map/convert_element_type | solution.py:476
Async XLA Ops:
  1.5 16.2 %all-to-all-start = ((bf16[8,128,128]{2,1,0:T(8,128)(2,1)}), bf16[8,128,128]{2,1,0:T(8,128)(2,1)S(1)}, u32[]{:S(2)}, u32[]{:S(2)}) async-start(bf16[8,128,128]{2,1,0:T(8,128)(2,1)} %broadcast_in_dim.2), calls=%async_computation | async-start | bytes 524288 | tf_op jit(solution)/shard_map/all_to_all | solution.py:389
  17.7 22.6 %copy-start = (bf16[2048,1024]{1,0:T(8,128)(2,1)S(1)}, bf16[2048,1024]{1,0:T(8,128)(2,1)}, u32[]{:S(2)}) copy-start(bf16[2048,1024]{1,0:T(8,128)(2,1)} %weight.1) | copy-start | bytes 12582916
  41.1 3.7 %collective-permute-start = (bf16[16,1024]{1,0:T(8,128)(2,1)S(1)}, bf16[16,1024]{1,0:T(8,128)(2,1)S(1)}, u32[]{:S(2)}, u32[]{:S(2)}) collective-permute-start(bf16[16,1024]{1,0:T(8,128)(2,1)S(1)} %get-tuple-element.28), channel_id=1, source_target_pairs={{0,3},{1,2},{2,1},{3,0},{4,7},{5,6},{6,5},{7,4},{8,11},{9,10},{10,... | collective-permute-start | bytes 98312 | tf_op jit(solution)/shard_map/ppermute | solution.py:475
  41.2 4.0 %collective-permute-start.1 = (bf16[16,1024]{1,0:T(8,128)(2,1)S(1)}, bf16[16,1024]{1,0:T(8,128)(2,1)S(1)}, u32[]{:S(2)}, u32[]{:S(2)}) collective-permute-start(bf16[16,1024]{1,0:T(8,128)(2,1)S(1)} %get-tuple-element.29), channel_id=1, source_target_pairs={{0,2},{1,3},{2,0},{3,1},{4,6},{5,7},{6,4},{7,5},{8,10},{9,11},{10,... | collective-permute-start | bytes 98312 | tf_op jit(solution)/shard_map/ppermute | solution.py:475
  42.8 2.5 %collective-permute-start.2 = (bf16[16,1024]{1,0:T(8,128)(2,1)S(1)}, bf16[16,1024]{1,0:T(8,128)(2,1)S(1)}, u32[]{:S(2)}, u32[]{:S(2)}) collective-permute-start(bf16[16,1024]{1,0:T(8,128)(2,1)S(1)} %get-tuple-element.30), channel_id=1, source_target_pairs={{0,1},{1,0},{2,3},{3,2},{4,5},{5,4},{6,7},{7,6},{8,9},{9,8},{10,11... | collective-permute-start | bytes 98312 | tf_op jit(solution)/shard_map/ppermute | solution.py:475

commit v7 on v6

--- a/solution.py
+++ b/solution.py
@@ -15,7 +15,7 @@
 pad_heads = 16
 stat_lanes = 16
 batch = 8
-batches = (24,)
+batches = (16, 24, 32, 40)
 sequence_unit = 1 << 10
 item_unit = 1 << 22
 early_bytes = 3 << 20
@@ -146,7 +146,22 @@
         page = lanes
         me = lax.axis_index("dp")
 
+        def page_copy(place):
+            item = page_list[place] // item_unit
+            return pltpu.make_async_copy(overflow.at[item], pages.at[place], sems.at[place])
+
+        def start_copy(place, _):
+            page_copy(place).start()
+            return 0
+
+        def end_copy(place, _):
+            page_copy(place).wait()
+            return 0
+
+        early = pages.shape[0]
+
         def scan_group(group, found):
+            before = jnp.minimum(found, early)
             slot = jnp.int32(0)
             holder_counts[group] = 0
             for row in range(seq_dev):
@@ -159,25 +174,13 @@
                     page_list[found] = slot * item_unit + (label + tokens)
                     slot = slot + named.astype(jnp.int32)
                     found = found + (named & (tokens > 0)).astype(jnp.int32)
+            lax.fori_loop(before, jnp.minimum(found, early), start_copy, 0)
             return found
 
         found_count = lax.fori_loop(0, group_count, scan_group, jnp.int32(0))
         page_count[0] = found_count
 
-        def page_copy(place):
-            item = page_list[place] // item_unit
-            return pltpu.make_async_copy(overflow.at[item], pages.at[place], sems.at[place])
-
-        def start_copy(place, _):
-            page_copy(place).start()
-            return 0
-
-        def end_copy(place, _):
-            page_copy(place).wait()
-            return 0
-
-        early_count = jnp.minimum(found_count, pages.shape[0])
-        lax.fori_loop(0, early_count, start_copy, 0)
+        early_count = jnp.minimum(found_count, early)
         home_copy.wait()
         for row in range(seq_dev):
             length = lengths[me * seq_dev + row]

time: 46.3 us -> 46.8 us (1.011)
  blocking collectives: 19.9 us -> 21.3 us
  Pallas kernels: 8.72 us -> 8.01 us
    all_to_all x1, blocking collectives: 10.1 us -> 11.6 us  [body(): lax.all_to_all(partials, 'dp', split_axis=0, concat_axis=0, tiled=True)]
    pallas_call x1, Pallas kernels: 2.23 us -> 1.51 us  [body(): pl.pallas_call(page_kernel, out_shape=near((group_count, slots + 1, 8, la...]
where the time goes in v7:
time: 46.8 us; the launch traced here: 46.6 us
  blocking collectives  21.3 us (46%)
  starting transfers between devices  9.23 us (20%)
  Pallas kernels  8.01 us (17%)
  waiting for transfers between devices  5.89 us (13%)
  local copies, waits for them, and re-layouts  1.49 us (3%)
  other arithmetic  0.64 us (1%)
    all_to_all x1, blocking collectives, body(): lax.all_to_all(partials, 'dp', split_axis=0, concat_axis=0, tiled=True)  11.6 us
    all_to_all x1, blocking collectives, body(): lax.all_to_all(merged, 'dp', split_axis=0, concat_axis=0, tiled=True)  9.74 us
    all_to_all x1, starting transfers between devices, body(): lax.all_to_all(spread_queries, 'dp', split_axis=0, concat_axis=0, tiled=T...  7.31 us
    pallas_call x1, Pallas kernels, body(): pl.pallas_call(home_kernel, out_shape=(ints(items + 1), ints(1), ints(ent...  5.2 us
    all_to_all x1, waiting for transfers between devices, body(): lax.all_to_all(spread_queries, 'dp', split_axis=0, concat_axis=0, tiled=T...  3.71 us
    ppermute x3, waiting for transfers between devices, body(): total = total + lax.ppermute(pieces[step], 'mp', ring).astype(f32)  2.18 us
    ppermute x3, starting transfers between devices, body(): total = total + lax.ppermute(pieces[step], 'mp', ring).astype(f32)  1.92 us
    pallas_call x1, Pallas kernels, body(): pl.pallas_call(page_kernel, out_shape=near((group_count, slots + 1, 8, la...  1.51 us
  transfers between devices with their start and end apart: 4, of which 3 were waited for; matrix products, arithmetic and copies ran while one was open for 0% of the time, Pallas kernels for 11%

profile of v7, /device:TPU:0, one launch (start us, length us, event | category | flops | bytes accessed | tf_op | source)
XLA Modules:
  0.0 46.6 jit_solution(12974655277471432577)
XLA Ops:
  0.0 1.5 %broadcast_in_dim.2 = bf16[8,128,128]{2,1,0:T(8,128)(2,1)} broadcast(bf16[128,128]{1,0:T(8,128)(2,1)} %bitcast.10), dimensions={1,2} | broadcast | bytes 294912 | tf_op jit(solution)/shard_map/broadcast_in_dim | solution.py:389
  1.5 7.3 %all-to-all-start = ((bf16[8,128,128]{2,1,0:T(8,128)(2,1)}), bf16[8,128,128]{2,1,0:T(8,128)(2,1)S(1)}, u32[]{:S(2)}, u32[]{:S(2)}) async-start(bf16[8,128,128]{2,1,0:T(8,128)(2,1)} %broadcast_in_dim.2), calls=%async_computation | async-start | bytes 524288 | tf_op jit(solution)/shard_map/all_to_all | solution.py:392
  8.8 5.2 %shard_map.82 = (s32[65]{0:T(128)S(4)}, s32[1]{0:T(128)S(4)}, s32[48]{0:T(128)S(4)}, s32[48]{0:T(128)S(4)}, f32[8,8,128]{2,1,0:T(8,128)S(1)}, /*index=5*/f32[8,8...) custom-call(s32[6,1,64]{2,1,0:T(1,128)} %bitcast.13, ...), custom_call_target="tpu_custom_call" | custom-call | flops 200000000 | bytes 1048576 | tf_op jit(solution)/shard_map/pallas_call | solution.py:402
  14.0 3.7 %all-to-all-done = bf16[8,128,128]{2,1,0:T(8,128)(2,1)S(1)} async-done(((bf16[8,128,128]{2,1,0:T(8,128)(2,1)}), bf16[8,128,128]{2,1,0:T(8,128)(2,1)S(1)}, u32[]{:S(2)}, u32[]{:S(2)}) %all-to-all-start) | async-done | bytes 262176 | tf_op jit(solution)/shard_map/all_to_all | solution.py:392
  17.7 0.0 copy-start
  17.7 1.5 %shard_map.83 = bf16[8,9,8,128]{3,2,1,0:T(8,128)(2,1)S(1)} custom-call(s32[65]{0:T(128)S(4)} %get-tuple-element.20.page_list, s32[1]{0:T(128)S(4)} %get-tuple-element.21.page_count, bf16[1024,128]{1,0:T(8,128)(2,1)S(1)} %bitcast.6, bf16[128,128]{1,0:T(8,128)(2,1)S(1)} %get-tuple-element.22.key_up, bf16[48,256,128]{2,1,0:T(8,128)(2,1)S(1)} %get-tuple-element.23.pages, ...), custom_call_target="tpu_custom_call" | custom-call | tf_op jit(solution)/shard_map/pallas_call | solution.py:436
  19.2 11.6 %all_to_all.15.received = bf16[8,9,8,128]{3,2,1,0:T(8,128)(2,1)S(1)} all-to-all(bf16[8,9,8,128]{3,2,1,0:T(8,128)(2,1)S(1)} %shard_map.83), channel_id=1, replica_groups=mesh['dp'=8,'mp'=4] {'dp'}, dimensions={0} | all-to-all | bytes 294912 | tf_op jit(solution)/shard_map/all_to_all | solution.py:450
  30.8 0.5 shard_map.84
  31.3 9.7 %all_to_all.16.received = bf16[8,8,8,128]{3,2,1,0:T(8,128)(2,1)S(1)} all-to-all(bf16[8,8,8,128]{3,2,1,0:T(8,128)(2,1)S(1)} %shard_map.84), channel_id=1, replica_groups=mesh['dp'=8,'mp'=4] {'dp'}, dimensions={0} | all-to-all | bytes 262144 | tf_op jit(solution)/shard_map/all_to_all | solution.py:460
  41.0 0.0 copy-done
  41.0 0.8 %shard_map.85 = (bf16[16,1024]{1,0:T(8,128)(2,1)S(1)}, bf16[16,1024]{1,0:T(8,128)(2,1)S(1)}, bf16[16,1024]{1,0:T(8,128)(2,1)S(1)}, bf16[16,1024]{1,0:T(8,128)(2,1)S(1)}) custom-call(bf16[8,8,8,128]{3,2,1,0:T(8,128)(2,1)S(1)} %all_to_all.16.received, bf16[2,64,128]{2,1,0:T(8,128)(2,1)S(1)} %get-tuple-element.26.value_up, bf16[2048,1024]{1,0:T(8,128)(2,1)S(1)} %copy-done), custom_call_target="tpu_custom_call" | custom-call | tf_op jit(solution)/shard_map/pallas_call | solution.py:465
  41.9 0.1 collective-permute-start
  42.0 1.6 %collective-permute-start.1 = (bf16[16,1024]{1,0:T(8,128)(2,1)S(1)}, bf16[16,1024]{1,0:T(8,128)(2,1)S(1)}, u32[]{:S(2)}, u32[]{:S(2)}) collective-permute-start(bf16[16,1024]{1,0:T(8,128)(2,1)S(1)} %get-tuple-element.29), channel_id=1, source_target_pairs={{0,2},{1,3},{2,0},{3,1},{4,6},{5,7},{6,4},{7,5},{8,10},{9,11},{10,... | collective-permute-start | bytes 98312 | tf_op jit(solution)/shard_map/ppermute | solution.py:478
  43.5 0.3 collective-permute-start.2
  43.8 1.8 %collective-permute-done = bf16[16,1024]{1,0:T(8,128)(2,1)S(1)} collective-permute-done((bf16[16,1024]{1,0:T(8,128)(2,1)S(1)}, bf16[16,1024]{1,0:T(8,128)(2,1)S(1)}, u32[]{:S(2)}, u32[]{:S(2)}) %collective-permute-start) | collective-permute-done | bytes 32800 | tf_op jit(solution)/shard_map/ppermute | solution.py:478
  45.6 0.4 collective-permute-done.1
  46.0 0.0 collective-permute-done.2
  46.0 0.6 %add_convert_fusion = bf16[16,1024]{1,0:T(8,128)(2,1)} fusion(bf16[16,1024]{1,0:T(8,128)(2,1)S(1)} %collective-permute-done.2, bf16[16,1024]{1,0:T(8,128)(2,1)S(1)} %collective-permute-done.1, bf16[16,1024]{1,0:T(8,128)(2,1)S(1)} %collective-permute-done, bf16[16,1024]{1,0:T(8,128)(2,1)S(1)} %get-tuple-element.27), kind=kLoop, calls=%fused_computation | loop fusion | flops 131072 | bytes 163840 | tf_op jit(solution)/shard_map/convert_element_type | solution.py:479
Async XLA Ops:
  1.5 16.2 %all-to-all-start = ((bf16[8,128,128]{2,1,0:T(8,128)(2,1)}), bf16[8,128,128]{2,1,0:T(8,128)(2,1)S(1)}, u32[]{:S(2)}, u32[]{:S(2)}) async-start(bf16[8,128,128]{2,1,0:T(8,128)(2,1)} %broadcast_in_dim.2), calls=%async_computation | async-start | bytes 524288 | tf_op jit(solution)/shard_map/all_to_all | solution.py:392
  17.7 23.3 %copy-start = (bf16[2048,1024]{1,0:T(8,128)(2,1)S(1)}, bf16[2048,1024]{1,0:T(8,128)(2,1)}, u32[]{:S(2)}) copy-start(bf16[2048,1024]{1,0:T(8,128)(2,1)} %weight.1) | copy-start | bytes 12582916
  41.9 3.7 %collective-permute-start = (bf16[16,1024]{1,0:T(8,128)(2,1)S(1)}, bf16[16,1024]{1,0:T(8,128)(2,1)S(1)}, u32[]{:S(2)}, u32[]{:S(2)}) collective-permute-start(bf16[16,1024]{1,0:T(8,128)(2,1)S(1)} %get-tuple-element.28), channel_id=1, source_target_pairs={{0,3},{1,2},{2,1},{3,0},{4,7},{5,6},{6,5},{7,4},{8,11},{9,10},{10,... | collective-permute-start | bytes 98312 | tf_op jit(solution)/shard_map/ppermute | solution.py:478
  42.0 4.0 %collective-permute-start.1 = (bf16[16,1024]{1,0:T(8,128)(2,1)S(1)}, bf16[16,1024]{1,0:T(8,128)(2,1)S(1)}, u32[]{:S(2)}, u32[]{:S(2)}) collective-permute-start(bf16[16,1024]{1,0:T(8,128)(2,1)S(1)} %get-tuple-element.29), channel_id=1, source_target_pairs={{0,2},{1,3},{2,0},{3,1},{4,6},{5,7},{6,4},{7,5},{8,10},{9,11},{10,... | collective-permute-start | bytes 98312 | tf_op jit(solution)/shard_map/ppermute | solution.py:478
  43.5 2.5 %collective-permute-start.2 = (bf16[16,1024]{1,0:T(8,128)(2,1)S(1)}, bf16[16,1024]{1,0:T(8,128)(2,1)S(1)}, u32[]{:S(2)}, u32[]{:S(2)}) collective-permute-start(bf16[16,1024]{1,0:T(8,128)(2,1)S(1)} %get-tuple-element.30), channel_id=1, source_target_pairs={{0,1},{1,0},{2,3},{3,2},{4,5},{5,4},{6,7},{7,6},{8,9},{9,8},{10,11... | collective-permute-start | bytes 98312 | tf_op jit(solution)/shard_map/ppermute | solution.py:478
